TPU v7x, 32 devices: a whole 2x2x4 slice. The times are simulated.
32 devices in a mesh: tm: 8 (over y, x, core), strip: 4 (over z).
Axes of the slice: x: 2, y: 2, z: 4, core: 2. Of those that a mesh axis runs over, the one named last changes fastest.
Arguments:
- signal: bfloat16 [2, 16, 16384], P(None, 'strip', 'tm'), may hold values from -5 to 5
Outputs:
- spectrum: bfloat16 [2, 256, 16, 8, 2048], P(None, 'strip', None, 'tm')
All inputs are finite; a program needn't handle non-finite values.
Results may differ from a plain program's by a relative error of at most 0.0069.
Values may be sent and summed in bfloat16 or wider, within the bound.
A program may use at most 128 MiB of HBM per device.

v0:
```python
import functools
import math

import jax
import jax.numpy as jnp
from jax import lax
from jax.experimental import pallas as pl
from jax.experimental.pallas import tpu as pltpu
from jax.sharding import PartitionSpec as P

K = 256
D = 8
EXTRA = 16
TWO_PI = 2.0 * math.pi


def unit_pair(phases, modulus):
    angles = jnp.float32(TWO_PI / modulus) * (phases % modulus).astype(jnp.float32)
    return jnp.cos(angles), jnp.sin(angles)


def channel_filters(channel_ids):
    offsets = jnp.arange(K, dtype=jnp.int32)
    cosine, sine = unit_pair(channel_ids[:, None] * offsets[None, :], K)
    hamming = 0.54 - 0.46 * jnp.cos(jnp.float32(TWO_PI) * offsets.astype(jnp.float32) / K)
    scaled = hamming[None, :] / math.sqrt(K)
    cosine = (scaled * cosine).astype(jnp.bfloat16)
    sine = (scaled * sine).astype(jnp.bfloat16)
    rows = []
    for real_taps, imag_taps in ((cosine, sine), (-sine, cosine)):
        for offset in range(D):
            pad = ((0, 0), (offset, EXTRA - offset))
            rows.append(
                jnp.concatenate([jnp.pad(real_taps, pad), jnp.pad(imag_taps, pad)], axis=1)
            )
    return jnp.concatenate(rows, axis=0)


def small_dft(values):
    count = len(values)
    if count == 1:
        return values
    even = small_dft(values[0::2])
    odd = small_dft(values[1::2])
    low, high = [], []
    for i in range(count // 2):
        er, ei = even[i]
        orr, oi = odd[i]
        if i == 0:
            tr, ti = orr, oi
        elif 4 * i == count:
            tr, ti = oi, -orr
        else:
            c = math.cos(TWO_PI * i / count)
            s = math.sin(TWO_PI * i / count)
            if abs(c - s) < 1e-6:
                tr, ti = (orr + oi) * c, (oi - orr) * c
            elif abs(c + s) < 1e-6:
                tr, ti = (oi - orr) * s, (orr + oi) * (-s)
            else:
                tr, ti = orr * c + oi * s, oi * c - orr * s
        low.append((er + tr, ei + ti))
        high.append((er - tr, ei - ti))
    return low + high


def make_body(blocks, piece, chan):
    total = blocks * piece
    rows = D * chan

    def body(x_ref, filt_ref, turn_ref, dft_ref, twid_ref, out_ref, taps_ref, acc_ref):
        parts = [x_ref[0, a, 0] for a in range(blocks)]
        parts.append(jnp.zeros((2 * D, 128), jnp.bfloat16))
        x = jnp.concatenate(parts, axis=1).astype(jnp.float32)
        width = total + 128
        span = K + EXTRA
        for c in range(2):
            base = x[c * D : (c + 1) * D]
            for q in range(0, span // D, 2):
                pair = []
                for s in (q, q + 1):
                    moved = base if s == 0 else pltpu.roll(base, width - s, 1)
                    pair.append(moved[:, :total])
                taps_ref[c * span + q * D : c * span + (q + 2) * D, :] = jnp.concatenate(
                    pair, axis=0
                ).astype(jnp.bfloat16)
        lag = K // 2 // D
        xr = pltpu.roll(x[:D], width - lag, 1)[:, :total]
        xi = pltpu.roll(x[D:], width - lag, 1)[:, :total]
        tc, ts = turn_ref[0], turn_ref[1]
        zr = xr * tc - xi * ts
        zi = -(xi * tc + xr * ts)
        for a in range(blocks):
            lanes = slice(a * piece, (a + 1) * piece)
            res = jnp.dot(
                filt_ref[...], taps_ref[:, lanes], preferred_element_type=jnp.float32
            )
            for o in range(D):
                r0 = o * chan
                fr = res[r0 : r0 + chan]
                fi = res[rows + r0 : rows + r0 + chan]
                br = zr[o : o + 1, lanes]
                bi = zi[o : o + 1, lanes]
                pr = fr * br - fi * bi
                pi = fr * bi + fi * br
                if a > 0:
                    pr = pr + acc_ref[r0 : r0 + chan]
                    pi = pi + acc_ref[rows + r0 : rows + r0 + chan]
                acc_ref[r0 : r0 + chan] = pr
                acc_ref[rows + r0 : rows + r0 + chan] = pi
        partial = jnp.concatenate(
            [acc_ref[:rows].astype(jnp.bfloat16), acc_ref[rows:].astype(jnp.bfloat16)], axis=1
        )
        inner = jnp.dot(partial, dft_ref[...], preferred_element_type=jnp.float32)
        turned = []
        for o in range(D):
            vr = inner[o * chan : (o + 1) * chan, :piece]
            vi = inner[o * chan : (o + 1) * chan, piece:]
            if o > 0:
                tc = twid_ref[0, o : o + 1]
                ts = twid_ref[1, o : o + 1]
                vr, vi = vr * tc + vi * ts, vi * tc - vr * ts
            turned.append((vr, vi))
        for m, (yr, yi) in enumerate(small_dft(turned)):
            out_ref[0, 0, :, m * piece : (m + 1) * piece] = yr.astype(jnp.bfloat16)
            out_ref[0, 1, :, m * piece : (m + 1) * piece] = yi.astype(jnp.bfloat16)

    return body


def gather_body(names, strips, blocks):
    count = strips * blocks

    def body(local_ref, every_ref, local_sem, send_sem, recv_sem):
        strip = lax.axis_index("strip")
        block = lax.axis_index("tm")
        me = strip * blocks + block

        def peer(step):
            other = lax.rem(me + step, count)
            where = {"strip": lax.div(other, blocks), "tm": lax.rem(other, blocks)}
            return tuple(where[name] for name in names)

        barrier = pltpu.get_barrier_semaphore()
        for step in range(1, count):
            pl.semaphore_signal(
                barrier, inc=1, device_id=peer(step), device_id_type=pl.DeviceIdType.MESH
            )
        own = pltpu.make_async_copy(local_ref, every_ref.at[strip, block], local_sem)
        own.start()
        pl.semaphore_wait(barrier, count - 1)
        copies = []
        for step in range(1, count):
            copy = pltpu.make_async_remote_copy(
                src_ref=local_ref,
                dst_ref=every_ref.at[strip, block],
                send_sem=send_sem.at[step - 1],
                recv_sem=recv_sem.at[step - 1],
                device_id=peer(step),
                device_id_type=pl.DeviceIdType.MESH,
            )
            copy.start()
            copies.append(copy)
        own.wait()
        for copy in copies:
            copy.wait()

    return body


def gather_everywhere(local, names, strips, blocks):
    return pl.pallas_call(
        gather_body(names, strips, blocks),
        out_shape=jax.ShapeDtypeStruct((strips, blocks) + local.shape, local.dtype),
        in_specs=[pl.BlockSpec(memory_space=pltpu.VMEM)],
        out_specs=pl.BlockSpec(memory_space=pl.ANY),
        scratch_shapes=[pltpu.SemaphoreType.DMA] + [pltpu.SemaphoreType.DMA((strips * blocks - 1,))] * 2,
        compiler_params=pltpu.CompilerParams(collective_id=0, has_side_effects=True),
        name="gather_everywhere",
    )(local)


def per_device(names, signal):
    blocks = lax.axis_size("tm")
    strips = lax.axis_size("strip")
    wloc, block_len = signal.shape[1], signal.shape[2]
    windows = wloc * strips
    piece = block_len // D
    chan = K // strips
    total = block_len * blocks
    span = K + EXTRA
    local = signal.reshape(2, wloc, piece, D).transpose(1, 0, 3, 2).reshape(wloc, 2 * D, piece)
    every = gather_everywhere(local, names, strips, blocks)
    channel_ids = lax.axis_index("strip") * chan + jnp.arange(chan, dtype=jnp.int32)
    filters = channel_filters(channel_ids)
    residue = lax.axis_index("tm")
    offs = jnp.arange(D, dtype=jnp.int32)
    samples = offs[:, None] + D * jnp.arange(piece * blocks, dtype=jnp.int32)[None, :]
    turn = jnp.stack(unit_pair(residue * samples, total)) * (1.0 / math.sqrt(blocks))
    ids = jnp.arange(piece, dtype=jnp.int32)
    dc, ds = unit_pair(ids[:, None] * ids[None, :], piece)
    dft = jnp.concatenate(
        [jnp.concatenate([dc, -ds], axis=1), jnp.concatenate([ds, dc], axis=1)], axis=0
    ) * (1.0 / math.sqrt(block_len))
    dft = dft.astype(jnp.bfloat16)
    twid = jnp.stack(unit_pair(offs[:, None] * ids[None, :], block_len))

    fixed = lambda *dims: pl.BlockSpec(dims, lambda w: (0,) * len(dims))
    out = pl.pallas_call(
        make_body(blocks, piece, chan),
        grid=(windows,),
        in_specs=[
            pl.BlockSpec((1, blocks, 1, 2 * D, piece), lambda w: (w // wloc, 0, w % wloc, 0, 0)),
            fixed(2 * D * chan, 2 * span),
            fixed(2, D, piece * blocks),
            fixed(2 * piece, 2 * piece),
            fixed(2, D, piece),
        ],
        out_specs=pl.BlockSpec((1, 2, chan, block_len), lambda w: (w, 0, 0, 0)),
        out_shape=jax.ShapeDtypeStruct((windows, 2, chan, block_len), jnp.bfloat16),
        scratch_shapes=[
            pltpu.VMEM((2 * span, piece * blocks), jnp.bfloat16),
            pltpu.VMEM((2 * D * chan, piece), jnp.float32),
        ],
        compiler_params=pltpu.CompilerParams(
            dimension_semantics=("arbitrary",), vmem_limit_bytes=56 * 1024 * 1024
        ),
        name="strip_windows",
    )(every, filters, turn, dft, twid)
    return out.transpose(1, 2, 0, 3).reshape(2, chan, windows, 1, block_len)


def solution(mesh):
    return jax.shard_map(
        functools.partial(per_device, tuple(mesh.axis_names)),
        mesh=mesh,
        in_specs=(P(None, "strip", "tm"),),
        out_specs=P(None, "strip", None, "tm", None),
        check_vma=False,
    )
```

profile of v0, /device:TPU:15, one launch (start us, length us, event | category | flops | bytes accessed | tf_op | source)
XLA Modules:
  0.0 131.0 jit_solution(14385927971465873206)
XLA Ops:
  0.0 0.0 copy-start.1
  0.1 0.1 fusion.75
  0.1 0.6 pad_maximum_fusion.twid_ref
  0.7 0.3 fusion.77
  1.1 0.3 multiply_convert_fusion.1
  1.4 0.3 fusion.68
  1.7 0.7 maximum_multiply_fusion.1.turn_ref
  2.4 1.0 fusion.25
  3.3 0.2 fusion.78
  3.5 0.0 copy-done.1
  3.5 0.6 reshape.198
  4.1 0.8 copy.4
  4.9 1.0 fusion.23
  6.0 0.9 fusion.dft_ref
  6.8 30.4 %gather_everywhere.1.x_ref = bf16[4,8,4,16,256]{4,3,2,1,0:T(8,128)(2,1)} custom-call(bf16[4,16,256]{2,1,0:T(8,128)(2,1)} %bitcast.7), custom_call_target="tpu_custom_call" | custom-call | tf_op jit(solution)/shard_map/gather_everywhere/pallas_call | solution.py:172
  37.3 0.1 fusion.27
  37.4 0.1 fusion.29
  37.5 0.1 fusion.31
  37.6 0.1 fusion.33
  37.7 0.1 fusion.35
  37.8 0.1 fusion.37
  37.8 0.1 fusion.39
  37.9 0.1 fusion.41
  38.0 0.1 fusion.43
  38.1 0.1 fusion.45
  38.2 0.1 fusion.47
  38.3 0.1 fusion.49
  38.5 0.1 fusion.51
  38.6 0.1 fusion.53
  38.7 0.1 fusion.55
  38.8 0.1 fusion.57.filt_ref
  38.9 0.0 copy-start
  38.9 1.0 copy-done
  39.9 79.7 %strip_windows.1 = bf16[16,2,64,2048]{3,2,1,0:T(8,128)(2,1)} custom-call(bf16[4,8,4,16,256]{4,3,2,1,0:T(8,128)(2,1)} %gather_everywhere.1.x_ref, bf16[1024,544]{1,0:T(8,128)(2,1)} %copy-done, f32[2,8,2048]{2,1,0:T(8,128)} %maximum_multiply_fusion.1.turn_ref, bf16[512,512]{1,0:T(8,128)(2,1)} %fusion.dft_ref, f32[2,8,256]{2,1,0:T(8,128)} %pad_maximum_fusion.twid_ref), custom_call_target="tpu_custom_call" | custom-call | tf_op jit(solution)/shard_map/strip_windows/pallas_call | solution.py:209
  119.6 11.4 %copy.5 = bf16[2,64,16,1,2048]{4,2,3,1,0:T(8,128)(2,1)} copy(bf16[2,64,16,1,2048]{4,1,0,2,3:T(8,128)(2,1)} %bitcast.5) | data formatting | bytes 16777216 | tf_op jit(solution)/shard_map/reshape | solution.py:230
  (3 shorter events, 0.1 us)
Async XLA Ops:
  0.0 3.5 %copy-start.1 = (bf16[2,4,2048]{2,1,0:T(4,128)(2,1)S(1)}, bf16[2,4,2048]{2,1,0:T(4,128)(2,1)}, u32[]{:S(2)}) copy-start(bf16[2,4,2048]{2,1,0:T(4,128)(2,1)} %param.1) | copy-start | bytes 98308
  38.9 1.1 copy-start
where the time goes:
time: 131 us
  Pallas kernels  110 us (84%)
  local copies, waits for them, and re-layouts  14 us (11%)
  other arithmetic  6.72 us (5%)
    pallas_call x1, Pallas kernels, per_device(): pl.pallas_call(make_body(blocks, piece, chan), grid=(windows,), in_specs=...  79.7 us
    pallas_call x1, Pallas kernels, gather_everywhere(): pl.pallas_call(gather_body(names, strips, blocks), out_shape=jax.ShapeDty...  30.4 us
    reshape x1, local copies, waits for them, and re-layouts, per_device(): return out.transpose(1, 2, 0, 3).reshape(2, chan, windows, 1, block_len)  11.4 us

commit v1 on v0

v1 whole, which is shorter than its diff:
```python
import functools
import math

import jax
import jax.numpy as jnp
import numpy as np
from jax import lax
from jax.experimental import pallas as pl
from jax.experimental.pallas import tpu as pltpu
from jax.sharding import PartitionSpec as P

K = 256
J = 256
HALF = 128
ALT = 64
TWO_PI = 2.0 * math.pi


def pair(phases, modulus):
    angles = TWO_PI * (phases % modulus) / modulus
    return np.cos(angles), np.sin(angles)


def small_dft(values):
    count = len(values)
    if count == 1:
        return values
    even = small_dft(values[0::2])
    odd = small_dft(values[1::2])
    low, high = [], []
    for i in range(count // 2):
        er, ei = even[i]
        orr, oi = odd[i]
        if i == 0:
            tr, ti = orr, oi
        elif 4 * i == count:
            tr, ti = oi, -orr
        else:
            c = math.cos(TWO_PI * i / count)
            s = math.sin(TWO_PI * i / count)
            if abs(c - s) < 1e-6:
                tr, ti = (orr + oi) * c, (oi - orr) * c
            elif abs(c + s) < 1e-6:
                tr, ti = (oi - orr) * s, (orr + oi) * (-s)
            else:
                tr, ti = orr * c + oi * s, oi * c - orr * s
        low.append((er + tr, ei + ti))
        high.append((er - tr, ei - ti))
    return low + high


def tables(blocks, block_len):
    d = block_len // J
    slots = J // (2 * blocks)
    total = blocks * block_len
    scale = 1.0 / math.sqrt(total * K)
    order = (
        HALF * d * np.arange(2)[:, None, None]
        + np.arange(d)[None, :, None]
        + d * np.arange(HALF)[None, None, :]
    ).reshape(-1)
    residues = np.arange(blocks)
    c, s = pair(residues[:, None] * order[None, :], total)
    lanes = np.stack([c, -s], axis=1) * scale
    c, s = pair(residues[:, None] * residues[None, :], blocks)
    folds = np.stack([c, -s], axis=1)[..., None] * np.ones(128)
    lane = np.arange(J)
    slot_of = (lane % HALF) // blocks
    slot = (np.arange(J) // (2 * blocks))[:, None] == slot_of[None, :]
    j = np.arange(HALF)
    b = d * j[None, :] + np.arange(d)[:, None]
    row = np.arange(J)
    lag = (row[None, :, None] - b[:, None, :]) % K
    start = ALT * (j // blocks)
    inside = (row[:, None] - start[None, :]) % K
    late = inside[None] < (b - start[None, :])[:, None, :]
    weight = 0.54 - 0.46 * np.cos(TWO_PI * lag / K)
    weight = np.where(late, -weight, weight)
    chan = np.arange(K)
    c, s = pair(chan[:, None] * row[None, :], K)
    emat = np.stack([np.concatenate([c, s], 1), np.concatenate([-s, c], 1)])
    c, s = pair(chan[:, None] * (d * j)[None, :], K)
    c1, s1 = pair(chan[:, None] * np.ones((1, HALF), np.int64), K)
    phase = np.stack([c, s, c1, s1])
    c, s = pair(row[:, None] * row[None, :], J)
    dft = np.concatenate([np.concatenate([c, -s], 1), np.concatenate([s, c], 1)], 0)
    twid = np.stack(pair(np.arange(d)[:, None] * row[None, :], block_len))
    f32 = lambda v: np.asarray(v, np.float32)
    b16 = lambda v: np.asarray(np.asarray(v, np.float32), jnp.bfloat16)
    return dict(
        lanes=f32(lanes), folds=f32(folds), slot=b16(slot), weight=f32(weight),
        emat=b16(emat), phase=f32(phase), dft=b16(dft), twid=f32(twid),
    )


def main_body(windows, blocks, block_len, chan, group):
    d = block_len // J
    ca = 2 * blocks
    slots = J // ca
    halves = block_len // 2
    rows = group * windows

    def body(
        xn_ref, zs_ref, slot_ref, weight_ref, dft_ref, twid_ref,
        lanes_hbm, folds_hbm, emat_hbm, phase_hbm, out_hbm,
        lanes_ref, folds_ref, emat_ref, phase_ref, turn_ref, spin_ref,
        lhs_ref, g_ref, out_ref, load_sem, out_sem,
    ):
        p = lax.axis_index("tm")
        s = lax.axis_index("strip")
        loads = [
            pltpu.make_async_copy(lanes_hbm.at[p], lanes_ref, load_sem.at[0]),
            pltpu.make_async_copy(folds_hbm.at[p], folds_ref, load_sem.at[1]),
            pltpu.make_async_copy(emat_hbm.at[:, pl.ds(s * chan, chan)], emat_ref, load_sem.at[2]),
            pltpu.make_async_copy(phase_hbm.at[:, pl.ds(s * chan, chan)], phase_ref, load_sem.at[3]),
        ]
        for load in loads:
            load.start()
        for load in loads:
            load.wait()
        br, bi = lanes_ref[0:1], lanes_ref[1:2]
        for q in range(block_len // 128):
            at = slice(q * 128, (q + 1) * 128)
            fr, fi = folds_ref[0], folds_ref[1]
            turn_ref[0, :, at] = fr * br[:, at] - fi * bi[:, at]
            turn_ref[1, :, at] = fr * bi[:, at] + fi * br[:, at]
        gr, gi = phase_ref[0], phase_ref[1]
        for o in range(d):
            if o > 0:
                gr, gi = gr * phase_ref[2] - gi * phase_ref[3], gr * phase_ref[3] + gi * phase_ref[2]
            spin_ref[o, 0] = gr
            spin_ref[o, 1] = gi

        low = lax.broadcasted_iota(jnp.int32, (ca, HALF), 1) < ALT
        emat = emat_ref[...].reshape(2 * chan, 2 * J)

        @pl.loop(0, windows)
        def _(w):
            def lane_tile(v):
                return xn_ref[w, :, v * 128 : (v + 1) * 128].astype(jnp.float32)

            for h in range(2):
                left, right, late = [], [], []
                for slot in range(slots):
                    g = (HALF * d * h) // ALT + slot
                    picks = []
                    for c in range(4):
                        n = g + (c - g) % 4
                        picks.append(n // 2)
                    for side, dst in ((0, left), (1, right)):
                        v0, v1 = picks[2 * side], picks[2 * side + 1]
                        x0 = lane_tile(v0)
                        dst.append(x0 if v0 == v1 else jnp.where(low, x0, lane_tile(v1)))
                    n = g + 4
                    tail = lane_tile(n // 2)
                    if n % 2:
                        tail = pltpu.roll(tail, ALT, 1)
                    late.append(-tail)
                lhs_ref[h, 0:ALT] = jnp.concatenate(late, axis=0).T[:ALT].astype(jnp.bfloat16)
                lhs_ref[h, ALT : ALT + HALF] = jnp.concatenate(left, axis=0).T.astype(jnp.bfloat16)
                lhs_ref[h, ALT + HALF :] = jnp.concatenate(right, axis=0).T.astype(jnp.bfloat16)

            for h in range(2):
                for o in range(0, d, 2):
                    at = slice(h * halves + o * HALF, h * halves + (o + 2) * HALF)
                    xs = zs_ref[w, :, at].astype(jnp.float32)
                    xr, xi = xs[:blocks], xs[blocks:]
                    er, ei = turn_ref[0, :, at], turn_ref[1, :, at]
                    zr = xr * er + xi * ei
                    zi = xr * ei - xi * er
                    mask = slot_ref[...]
                    zre = jnp.concatenate([zr, -zi], axis=0).astype(jnp.bfloat16)
                    zim = jnp.concatenate([zi, zr], axis=0).astype(jnp.bfloat16)
                    rhs = jnp.concatenate(
                        [
                            jnp.concatenate([zre] * slots, axis=0) * mask,
                            jnp.concatenate([zim] * slots, axis=0) * mask,
                        ],
                        axis=1,
                    )
                    lags = jnp.dot(lhs_ref[h], rhs, preferred_element_type=jnp.float32)
                    cols = []
                    for c in range(2):
                        for oo in range(2):
                            lanes = slice(c * J + oo * HALF, c * J + (oo + 1) * HALF)
                            late = lags[:ALT, lanes]
                            parts = []
                            for q in range(4):
                                t = weight_ref[o + oo, q * ALT : (q + 1) * ALT]
                                early = lags[(q + 1) * ALT : (q + 2) * ALT, lanes]
                                parts.append((jnp.where(t > 0, early, late) * t).astype(jnp.bfloat16))
                            cols.append(jnp.concatenate(parts, axis=0))
                    taps = jnp.concatenate(
                        [jnp.concatenate(cols[:2], axis=1), jnp.concatenate(cols[2:], axis=1)], axis=0
                    )
                    y = jnp.dot(emat, taps, preferred_element_type=jnp.float32)
                    for oo in range(2):
                        lanes = slice(oo * HALF, (oo + 1) * HALF)
                        yr, yi = y[:chan, lanes], y[chan:, lanes]
                        c, sn = spin_ref[o + oo, 0], spin_ref[o + oo, 1]
                        g_ref[o + oo, h, pl.ds(w, chan, stride=windows), :] = yr * c - yi * sn
                        g_ref[o + oo, 2 + h, pl.ds(w, chan, stride=windows), :] = yr * sn + yi * c

        chunks = chan // group

        def write(i, slot):
            return pltpu.make_async_copy(
                out_ref.at[slot], out_hbm.at[:, pl.ds(i * group, group)], out_sem.at[slot]
            )

        step = min(2, group)

        @pl.loop(0, chunks)
        def _(i):
            slot = lax.rem(i, 2)

            @pl.when(i >= 2)
            def _():
                write(i - 2, slot).wait()

            for u in range(0, group, step):
                first = i * rows + u * windows
                count = step * windows
                lhs = jnp.concatenate(
                    [
                        jnp.concatenate(
                            [g_ref[o, e, pl.ds(first, count), :].astype(jnp.bfloat16) for e in range(4)],
                            axis=1,
                        )
                        for o in range(d)
                    ],
                    axis=0,
                )
                inner = jnp.dot(lhs, dft_ref[...], preferred_element_type=jnp.float32)
                turned = []
                for o in range(d):
                    vr = inner[o * count : (o + 1) * count, :J]
                    vi = inner[o * count : (o + 1) * count, J:]
                    if o > 0:
                        tc, ts = twid_ref[0, o : o + 1], twid_ref[1, o : o + 1]
                        vr, vi = vr * tc + vi * ts, vi * tc - vr * ts
                    turned.append((vr, vi))
                for m, (yr, yi) in enumerate(small_dft(turned)):
                    lanes = slice(m * J, (m + 1) * J)
                    out_ref[slot, 0, u : u + step, :, lanes] = yr.astype(jnp.bfloat16).reshape(step, windows, J)
                    out_ref[slot, 1, u : u + step, :, lanes] = yi.astype(jnp.bfloat16).reshape(step, windows, J)
            write(i, slot).start()

        for i in range(max(chunks - 2, 0), chunks):
            write(i, i % 2).wait()

    return body


def gather_body(names, strips, blocks):
    count = strips * blocks

    def body(local_ref, every_ref, local_sem, send_sem, recv_sem):
        strip = lax.axis_index("strip")
        block = lax.axis_index("tm")
        me = strip * blocks + block

        def peer(step):
            other = lax.rem(me + step, count)
            where = {"strip": lax.div(other, blocks), "tm": lax.rem(other, blocks)}
            return tuple(where[name] for name in names)

        barrier = pltpu.get_barrier_semaphore()
        for step in range(1, count):
            pl.semaphore_signal(
                barrier, inc=1, device_id=peer(step), device_id_type=pl.DeviceIdType.MESH
            )
        own = pltpu.make_async_copy(local_ref, every_ref.at[strip, block], local_sem)
        own.start()
        pl.semaphore_wait(barrier, count - 1)
        copies = []
        for step in range(1, count):
            copy = pltpu.make_async_remote_copy(
                src_ref=local_ref,
                dst_ref=every_ref.at[strip, block],
                send_sem=send_sem.at[step - 1],
                recv_sem=recv_sem.at[step - 1],
                device_id=peer(step),
                device_id_type=pl.DeviceIdType.MESH,
            )
            copy.start()
            copies.append(copy)
        own.wait()
        for copy in copies:
            copy.wait()

    return body


def gather_everywhere(local, names, strips, blocks):
    return pl.pallas_call(
        gather_body(names, strips, blocks),
        out_shape=jax.ShapeDtypeStruct((strips, blocks) + local.shape, local.dtype),
        in_specs=[pl.BlockSpec(memory_space=pltpu.VMEM)],
        out_specs=pl.BlockSpec(memory_space=pl.ANY),
        scratch_shapes=[pltpu.SemaphoreType.DMA] + [pltpu.SemaphoreType.DMA((strips * blocks - 1,))] * 2,
        compiler_params=pltpu.CompilerParams(collective_id=0, has_side_effects=True),
        name="gather_everywhere",
    )(local)


def per_device(names, signal):
    blocks = lax.axis_size("tm")
    strips = lax.axis_size("strip")
    wloc, block_len = signal.shape[1], signal.shape[2]
    windows = wloc * strips
    chan = K // strips
    d = block_len // J
    ca = 2 * blocks
    tab = tables(blocks, block_len)

    every = gather_everywhere(signal.reshape(2 * wloc, block_len), names, strips, blocks)
    x = every.reshape(strips, blocks, 2, wloc, block_len).transpose(0, 3, 2, 1, 4)
    x = x.reshape(windows, 2, blocks, block_len)
    halo = jnp.concatenate([x[:, :, 1:, :K], jnp.zeros((windows, 2, 1, K), x.dtype)], axis=2)
    xn = jnp.concatenate([x, halo], axis=3).reshape(windows, ca, block_len + K)
    zs = xn[:, :, K // 2 : K // 2 + block_len].reshape(windows, ca, 2, HALF, d)
    zs = zs.transpose(0, 1, 2, 4, 3).reshape(windows, ca, block_len)

    group = min(8, chan)
    vmem = pl.BlockSpec(memory_space=pltpu.VMEM)
    hbm = pl.BlockSpec(memory_space=pl.ANY)
    out = pl.pallas_call(
        main_body(windows, blocks, block_len, chan, group),
        in_specs=[vmem] * 6 + [hbm] * 4,
        out_specs=hbm,
        out_shape=jax.ShapeDtypeStruct((2, chan, windows, block_len), jnp.bfloat16),
        scratch_shapes=[
            pltpu.VMEM((2, block_len), jnp.float32),
            pltpu.VMEM((2, blocks, 128), jnp.float32),
            pltpu.VMEM((2, chan, 2 * J), jnp.bfloat16),
            pltpu.VMEM((4, chan, HALF), jnp.float32),
            pltpu.VMEM((2, blocks, block_len), jnp.float32),
            pltpu.VMEM((d, 2, chan, HALF), jnp.float32),
            pltpu.VMEM((2, ALT + J, J), jnp.bfloat16),
            pltpu.VMEM((d, 4, chan * windows, HALF), jnp.float32),
            pltpu.VMEM((2, 2, group, windows, block_len), jnp.bfloat16),
            pltpu.SemaphoreType.DMA((4,)),
            pltpu.SemaphoreType.DMA((2,)),
        ],
        compiler_params=pltpu.CompilerParams(vmem_limit_bytes=56 * 1024 * 1024),
        name="strip_windows",
    )(xn, zs, tab["slot"], tab["weight"], tab["dft"], tab["twid"],
      tab["lanes"], tab["folds"], tab["emat"], tab["phase"])
    return out.reshape(2, chan, windows, 1, block_len)


def solution(mesh):
    return jax.shard_map(
        functools.partial(per_device, tuple(mesh.axis_names)),
        mesh=mesh,
        in_specs=(P(None, "strip", "tm"),),
        out_specs=P(None, "strip", None, "tm", None),
        check_vma=False,
    )
```

time: 131 us -> 104 us (0.79)
  Pallas kernels: 110 us -> 83.5 us
  other arithmetic: 6.72 us -> 1.21 us
  local copies, waits for them, and re-layouts: 14 us -> 18.7 us
    pallas_call x1, Pallas kernels: 79.7 us -> 53 us  [per_device(): pl.pallas_call(main_body(windows, blocks, block_len, chan, group), in_spe...]
    transpose x1, local copies, waits for them, and re-layouts: 0.8 us -> 8.27 us  [per_device(): zs = zs.transpose(0, 1, 2, 4, 3).reshape(windows, ca, block_len)]
    reshape x2 -> x4, local copies, waits for them, and re-layouts: 12 us -> 4.7 us  [the longest x2 2.04 us: per_device(): every.reshape(strips, blocks, 2, wloc, block_len).transpose(0, 3, 2, 1, 4)]
    slice x0 -> x2, local copies, waits for them, and re-layouts: none -> 5.7 us  [the longest x1 5.67 us: per_device(): zs = xn[:, :, K // 2:K // 2 + block_len].reshape(windows, ca, 2, HALF, d)]
    unnamed x15 -> x0, other arithmetic: 1.42 us -> none
where the time goes in v1:
time: 104 us; the launch traced here: 103 us
  Pallas kernels  83.5 us (80%)
  local copies, waits for them, and re-layouts  18.7 us (18%)
  other arithmetic  1.21 us (1%)
    pallas_call x1, Pallas kernels, per_device(): pl.pallas_call(main_body(windows, blocks, block_len, chan, group), in_spe...  53 us
    pallas_call x1, Pallas kernels, gather_everywhere(): pl.pallas_call(gather_body(names, strips, blocks), out_shape=jax.ShapeDty...  30.4 us
    transpose x1, local copies, waits for them, and re-layouts, per_device(): zs = zs.transpose(0, 1, 2, 4, 3).reshape(windows, ca, block_len)  8.27 us
    slice x1, local copies, waits for them, and re-layouts, per_device(): zs = xn[:, :, K // 2:K // 2 + block_len].reshape(windows, ca, 2, HALF, d)  5.67 us

profile of v1, /device:TPU:15, one launch (start us, length us, event | category | flops | bytes accessed | tf_op | source)
XLA Modules:
  0.0 103.5 jit_solution(991794939041121768)
XLA Ops:
  0.0 1.4 %reshape.22.local_ref = bf16[8,2048]{1,0:T(8,128)(2,1)} reshape(bf16[2,4,2048]{2,1,0:T(4,128)(2,1)} %param.9) | data formatting | bytes 65536 | tf_op jit(solution)/shard_map/reshape | solution.py:317
  1.4 30.4 %gather_everywhere.1 = bf16[4,8,8,2048]{3,2,1,0:T(8,128)(2,1)} custom-call(bf16[8,2048]{1,0:T(8,128)(2,1)} %reshape.22.local_ref), custom_call_target="tpu_custom_call" | custom-call | tf_op jit(solution)/shard_map/gather_everywhere/pallas_call | solution.py:296
  31.8 1.5 %reshape.23 = bf16[4,8,2,4,2048]{4,3,2,1,0:T(4,128)(2,1)S(1)} reshape(bf16[4,8,8,2048]{3,2,1,0:T(8,128)(2,1)} %gather_everywhere.1) | data formatting | bytes 2097152 | tf_op jit(solution)/shard_map/reshape | solution.py:318
  33.3 0.6 copy.13
  34.0 0.1 fusion
  34.1 1.1 %pad_maximum_fusion.xn_ref = bf16[16,16,2304]{2,1,0:T(8,128)(2,1)} fusion(bf16[16,16,256]{2,1,0:T(8,128)(2,1)S(1)} %pad_bitcast_fusion, bf16[16,16,2048]{2,1,0:T(8,128)(2,1)S(1)} %bitcast.20), kind=kLoop, calls=%fused_computation.1 | loop fusion | flops 2359296 | bytes 2359296 | tf_op jit(solution)/shard_map/concatenate | solution.py:321
  35.2 5.7 %copy.14 = bf16[16,16,2048]{1,2,0:T(8,128)(2,1)} copy(bf16[16,16,2048]{2,1,0:T(8,128)(2,1)S(1)} %fusion) | data formatting | bytes 2097152 | tf_op jit(solution)/shard_map/slice | solution.py:322
  40.9 8.3 %copy.15 = bf16[16,16,2,8,128]{4,3,2,1,0:T(8,128)(2,1)S(1)} copy(bf16[16,16,2,8,128]{1,3,4,2,0:T(8,128)(2,1)} %bitcast.17) | data formatting | bytes 2097152 | tf_op jit(solution)/shard_map/transpose | solution.py:323
  49.1 1.3 %reshape.26.zs_ref = bf16[16,16,2048]{2,1,0:T(8,128)(2,1)} reshape(bf16[16,16,2,8,128]{4,3,2,1,0:T(8,128)(2,1)S(1)} %copy.15) | data formatting | bytes 2097152 | tf_op jit(solution)/shard_map/reshape | solution.py:323
  50.4 53.0 %strip_windows.1 = bf16[2,64,16,2048]{3,2,1,0:T(8,128)(2,1)} custom-call(bf16[16,16,2304]{2,1,0:T(8,128)(2,1)} %pad_maximum_fusion.xn_ref, bf16[16,16,2048]{2,1,0:T(8,128)(2,1)} %reshape.26.zs_ref, bf16[256,256]{1,0:T(8,128)(2,1)} %constant.18.clone.slot_ref, f32[8,256,128]{2,1,0:T(8,128)} %constant.19.clone.weight_ref, ...), custom_call_target="tpu_custom_call" | custom-call | tf_op jit(solution)/shard_map/strip_windows/pallas_call | solution.py:328
  (2 shorter events, 0.1 us)

commit v2 on v1

--- a/solution.py
+++ b/solution.py
@@ -13,6 +13,7 @@
 J = 256
 HALF = 128
 ALT = 64
+UNROLL = 2
 TWO_PI = 2.0 * math.pi
 
 
@@ -98,7 +99,7 @@
     ca = 2 * blocks
     slots = J // ca
     halves = block_len // 2
-    rows = group * windows
+    pitch = windows + 1
 
     def body(
         xn_ref, zs_ref, slot_ref, weight_ref, dft_ref, twid_ref,
@@ -134,19 +135,15 @@
         low = lax.broadcasted_iota(jnp.int32, (ca, HALF), 1) < ALT
         emat = emat_ref[...].reshape(2 * chan, 2 * J)
 
-        @pl.loop(0, windows)
-        def _(w):
+        def build(w, slot):
             def lane_tile(v):
                 return xn_ref[w, :, v * 128 : (v + 1) * 128].astype(jnp.float32)
 
             for h in range(2):
                 left, right, late = [], [], []
-                for slot in range(slots):
-                    g = (HALF * d * h) // ALT + slot
-                    picks = []
-                    for c in range(4):
-                        n = g + (c - g) % 4
-                        picks.append(n // 2)
+                for part in range(slots):
+                    g = (HALF * d * h) // ALT + part
+                    picks = [(g + (c - g) % 4) // 2 for c in range(4)]
                     for side, dst in ((0, left), (1, right)):
                         v0, v1 = picks[2 * side], picks[2 * side + 1]
                         x0 = lane_tile(v0)
@@ -156,50 +153,67 @@
                     if n % 2:
                         tail = pltpu.roll(tail, ALT, 1)
                     late.append(-tail)
-                lhs_ref[h, 0:ALT] = jnp.concatenate(late, axis=0).T[:ALT].astype(jnp.bfloat16)
-                lhs_ref[h, ALT : ALT + HALF] = jnp.concatenate(left, axis=0).T.astype(jnp.bfloat16)
-                lhs_ref[h, ALT + HALF :] = jnp.concatenate(right, axis=0).T.astype(jnp.bfloat16)
-
-            for h in range(2):
-                for o in range(0, d, 2):
-                    at = slice(h * halves + o * HALF, h * halves + (o + 2) * HALF)
-                    xs = zs_ref[w, :, at].astype(jnp.float32)
-                    xr, xi = xs[:blocks], xs[blocks:]
-                    er, ei = turn_ref[0, :, at], turn_ref[1, :, at]
-                    zr = xr * er + xi * ei
-                    zi = xr * ei - xi * er
-                    mask = slot_ref[...]
-                    zre = jnp.concatenate([zr, -zi], axis=0).astype(jnp.bfloat16)
-                    zim = jnp.concatenate([zi, zr], axis=0).astype(jnp.bfloat16)
-                    rhs = jnp.concatenate(
-                        [
-                            jnp.concatenate([zre] * slots, axis=0) * mask,
-                            jnp.concatenate([zim] * slots, axis=0) * mask,
-                        ],
-                        axis=1,
-                    )
-                    lags = jnp.dot(lhs_ref[h], rhs, preferred_element_type=jnp.float32)
-                    cols = []
-                    for c in range(2):
-                        for oo in range(2):
-                            lanes = slice(c * J + oo * HALF, c * J + (oo + 1) * HALF)
-                            late = lags[:ALT, lanes]
-                            parts = []
-                            for q in range(4):
-                                t = weight_ref[o + oo, q * ALT : (q + 1) * ALT]
-                                early = lags[(q + 1) * ALT : (q + 2) * ALT, lanes]
-                                parts.append((jnp.where(t > 0, early, late) * t).astype(jnp.bfloat16))
-                            cols.append(jnp.concatenate(parts, axis=0))
-                    taps = jnp.concatenate(
-                        [jnp.concatenate(cols[:2], axis=1), jnp.concatenate(cols[2:], axis=1)], axis=0
-                    )
-                    y = jnp.dot(emat, taps, preferred_element_type=jnp.float32)
-                    for oo in range(2):
-                        lanes = slice(oo * HALF, (oo + 1) * HALF)
-                        yr, yi = y[:chan, lanes], y[chan:, lanes]
-                        c, sn = spin_ref[o + oo, 0], spin_ref[o + oo, 1]
-                        g_ref[o + oo, h, pl.ds(w, chan, stride=windows), :] = yr * c - yi * sn
-                        g_ref[o + oo, 2 + h, pl.ds(w, chan, stride=windows), :] = yr * sn + yi * c
+                lhs_ref[slot, h, 0:ALT] = jnp.concatenate(late, axis=0).T[:ALT].astype(jnp.bfloat16)
+                lhs_ref[slot, h, ALT : ALT + HALF] = jnp.concatenate(left, axis=0).T.astype(jnp.bfloat16)
+                lhs_ref[slot, h, ALT + HALF :] = jnp.concatenate(right, axis=0).T.astype(jnp.bfloat16)
+
+        def lag_products(w, slot, h, o):
+            at = slice(h * halves + o * HALF, h * halves + (o + 2) * HALF)
+            xs = zs_ref[w, :, at].astype(jnp.float32)
+            xr, xi = xs[:blocks], xs[blocks:]
+            er, ei = turn_ref[0, :, at], turn_ref[1, :, at]
+            zr = xr * er + xi * ei
+            zi = xr * ei - xi * er
+            mask = slot_ref[...]
+            zre = jnp.concatenate([zr, -zi], axis=0).astype(jnp.bfloat16)
+            zim = jnp.concatenate([zi, zr], axis=0).astype(jnp.bfloat16)
+            rhs = jnp.concatenate(
+                [
+                    jnp.concatenate([zre] * slots, axis=0) * mask,
+                    jnp.concatenate([zim] * slots, axis=0) * mask,
+                ],
+                axis=1,
+            )
+            return jnp.dot(lhs_ref[slot, h], rhs, preferred_element_type=jnp.float32)
+
+        def channels(w, h, o, lags):
+            cols = []
+            for c in range(2):
+                for oo in range(2):
+                    lanes = slice(c * J + oo * HALF, c * J + (oo + 1) * HALF)
+                    late = lags[:ALT, lanes]
+                    parts = []
+                    for q in range(4):
+                        t = weight_ref[o + oo, q * ALT : (q + 1) * ALT]
+                        early = lags[(q + 1) * ALT : (q + 2) * ALT, lanes]
+                        parts.append((jnp.where(t > 0, early, late) * t).astype(jnp.bfloat16))
+                    cols.append(jnp.concatenate(parts, axis=0))
+            taps = jnp.concatenate(
+                [jnp.concatenate(cols[:2], axis=1), jnp.concatenate(cols[2:], axis=1)], axis=0
+            )
+            y = jnp.dot(emat, taps, preferred_element_type=jnp.float32)
+            for oo in range(2):
+                lanes = slice(oo * HALF, (oo + 1) * HALF)
+                yr, yi = y[:chan, lanes], y[chan:, lanes]
+                c, sn = spin_ref[o + oo, 0], spin_ref[o + oo, 1]
+                g_ref[o + oo, h, pl.ds(w, chan, stride=pitch), :] = yr * c - yi * sn
+                g_ref[o + oo, 2 + h, pl.ds(w, chan, stride=pitch), :] = yr * sn + yi * c
+
+        build(0, 0)
+
+        @pl.loop(0, windows // UNROLL)
+        def _(i):
+            pending = None
+            for u in range(UNROLL):
+                w = i * UNROLL + u
+                build(jnp.minimum(w + 1, windows - 1), (u + 1) % 2)
+                for h in range(2):
+                    for o in range(0, d, 2):
+                        lags = lag_products(w, u % 2, h, o)
+                        if pending is not None:
+                            channels(*pending)
+                        pending = (w, h, o, lags)
+            channels(*pending)
 
         chunks = chan // group
 
@@ -219,15 +233,18 @@
                 write(i - 2, slot).wait()
 
             for u in range(0, group, step):
-                first = i * rows + u * windows
                 count = step * windows
                 lhs = jnp.concatenate(
                     [
                         jnp.concatenate(
-                            [g_ref[o, e, pl.ds(first, count), :].astype(jnp.bfloat16) for e in range(4)],
+                            [
+                                g_ref[o, e, pl.ds((i * group + u + k) * pitch, windows), :].astype(jnp.bfloat16)
+                                for e in range(4)
+                            ],
                             axis=1,
                         )
                         for o in range(d)
+                        for k in range(step)
                     ],
                     axis=0,
                 )
@@ -252,56 +269,179 @@
     return body
 
 
-def gather_body(names, strips, blocks):
-    count = strips * blocks
-
-    def body(local_ref, every_ref, local_sem, send_sem, recv_sem):
-        strip = lax.axis_index("strip")
-        block = lax.axis_index("tm")
-        me = strip * blocks + block
-
-        def peer(step):
-            other = lax.rem(me + step, count)
-            where = {"strip": lax.div(other, blocks), "tm": lax.rem(other, blocks)}
+def gather_body(names, strips, blocks, wloc, block_len):
+    d = block_len // J
+    ca = 2 * blocks
+    pairs = blocks // 2
+    lanes_o = J // d
+    copies_sent = strips * blocks - 1
+
+    def body(
+        local_ref, rows_ref, lane_ref, xn_hbm, zs_hbm,
+        every_ref, xn_ref, zs_ref, own_sem, send_sem, recv_sem, store_sem,
+    ):
+        s = lax.axis_index("strip")
+        t = lax.axis_index("tm")
+        other = t + 1 - 2 * lax.rem(t, 2)
+
+        def device(strip, tm):
+            where = {"strip": strip, "tm": tm}
             return tuple(where[name] for name in names)
 
+        def strip_at(ds):
+            return lax.rem(s + strips - ds, strips)
+
+        def mate(dt):
+            return lax.rem(t + blocks - 2 * dt, blocks)
+
+        def rival(dt):
+            return lax.rem(other + blocks - 2 * dt, blocks)
+
+        across = [device(strip_at(strips - ds), t) for ds in range(1, strips)]
+        inside = [device(s, mate(dt)) for dt in range(1, pairs)] + [device(s, other)]
         barrier = pltpu.get_barrier_semaphore()
-        for step in range(1, count):
-            pl.semaphore_signal(
-                barrier, inc=1, device_id=peer(step), device_id_type=pl.DeviceIdType.MESH
-            )
-        own = pltpu.make_async_copy(local_ref, every_ref.at[strip, block], local_sem)
+        for peer in across + inside:
+            pl.semaphore_signal(barrier, inc=1, device_id=peer, device_id_type=pl.DeviceIdType.MESH)
+        own = pltpu.make_async_copy(local_ref, every_ref.at[s, t], own_sem)
         own.start()
-        pl.semaphore_wait(barrier, count - 1)
-        copies = []
-        for step in range(1, count):
+        pl.semaphore_wait(barrier, len(across) + len(inside))
+
+        sent = []
+
+        def send(src, strip, tm, peer):
             copy = pltpu.make_async_remote_copy(
-                src_ref=local_ref,
-                dst_ref=every_ref.at[strip, block],
-                send_sem=send_sem.at[step - 1],
-                recv_sem=recv_sem.at[step - 1],
-                device_id=peer(step),
+                src_ref=src,
+                dst_ref=every_ref.at[strip, tm],
+                send_sem=send_sem.at[len(sent)],
+                recv_sem=recv_sem.at[strip, tm],
+                device_id=peer,
                 device_id_type=pl.DeviceIdType.MESH,
             )
             copy.start()
-            copies.append(copy)
+            sent.append(copy)
+
+        def arrived(strip, tm):
+            pltpu.make_async_remote_copy(
+                src_ref=every_ref.at[strip, tm],
+                dst_ref=every_ref.at[strip, tm],
+                send_sem=send_sem.at[0],
+                recv_sem=recv_sem.at[strip, tm],
+                device_id=device(s, other),
+                device_id_type=pl.DeviceIdType.MESH,
+            ).wait_recv()
+
+        for peer in across + inside:
+            send(local_ref, s, t, peer)
+
+        def relay(ds):
+            arrived(strip_at(ds), t)
+            for peer in inside:
+                send(every_ref.at[strip_at(ds), t], strip_at(ds), t, peer)
+
+        def hand_over(ds):
+            for dt in range(1, pairs):
+                arrived(strip_at(ds), mate(dt))
+                send(every_ref.at[strip_at(ds), mate(dt)], strip_at(ds), mate(dt), device(s, other))
+
+        def store(ds, which):
+            at = pl.ds(strip_at(ds) * wloc, wloc)
+            src, dst = ((xn_ref, xn_hbm), (zs_ref, zs_hbm))[which]
+            return pltpu.make_async_copy(src.at[at], dst.at[at], store_sem.at[ds, which])
+
+        def arrange(ds):
+            for dt in range(pairs):
+                arrived(strip_at(ds), rival(dt))
+            first = strip_at(ds) * wloc
+            slabs = [
+                every_ref[strip_at(ds), a, c].astype(jnp.float32) for a in range(blocks) for c in range(2)
+            ]
+            flat = jnp.concatenate(slabs, axis=0).astype(jnp.bfloat16)
+            count = ca * wloc
+            nat = jnp.dot(rows_ref[0], flat, preferred_element_type=jnp.float32).astype(jnp.bfloat16)
+            halo = jnp.dot(rows_ref[1], flat[:, :K], preferred_element_type=jnp.float32).astype(jnp.bfloat16)
+            full = jnp.concatenate([nat, halo], axis=1)
+            for wl in range(wloc):
+                xn_ref[first + wl] = full[wl * ca : (wl + 1) * ca]
+            moved = jnp.concatenate(
+                [full[:, HALF + q * J : HALF + (q + 1) * J] for q in range(block_len // J)], axis=0
+            )
+            moved = jnp.dot(moved, lane_ref[...], preferred_element_type=jnp.float32)
+            for h in range(2):
+                for o in range(d):
+                    lanes = slice(o * lanes_o, (o + 1) * lanes_o)
+                    part = jnp.concatenate(
+                        [
+                            moved[q * count : (q + 1) * count, lanes]
+                            for q in range(h * d // 2, (h + 1) * d // 2)
+                        ],
+                        axis=1,
+                    ).astype(jnp.bfloat16)
+                    for wl in range(wloc):
+                        zs_ref[first + wl, :, (h * d + o) * HALF : (h * d + o + 1) * HALF] = part[
+                            wl * ca : (wl + 1) * ca
+                        ]
+            store(ds, 0).start()
+            store(ds, 1).start()
+
+        near = [1, strips - 1] if strips > 2 else [1]
+        far = [ds for ds in range(1, strips) if ds not in near]
+        for ds in near:
+            relay(ds)
+        hand_over(0)
+        for ds in far:
+            relay(ds)
         own.wait()
-        for copy in copies:
-            copy.wait()
+        arrange(0)
+        for ds in near + far:
+            hand_over(ds)
+            arrange(ds)
+        for copy in sent:
+            copy.wait_send()
+        for ds in range(strips):
+            store(ds, 0).wait()
+            store(ds, 1).wait()
 
     return body
 
 
-def gather_everywhere(local, names, strips, blocks):
+def gather_everywhere(signal, names, strips, blocks):
+    wloc, block_len = signal.shape[1], signal.shape[2]
+    d = block_len // J
+    windows = wloc * strips
+    ca = 2 * blocks
+    count = ca * wloc
+    lanes_o = J // d
+    w, c, a = np.meshgrid(np.arange(wloc), np.arange(2), np.arange(blocks), indexing="ij")
+    target = ((w * 2 + c) * blocks + a).reshape(-1)
+    source = ((a * 2 + c) * wloc + w).reshape(-1)
+    rows = np.zeros((2, count, count))
+    rows[0, target, source] = 1.0
+    inner = a.reshape(-1) + 1 < blocks
+    rows[1, target[inner], source[inner] + 2 * wloc] = 1.0
+    lane = np.zeros((J, J))
+    n = np.arange(J)
+    lane[n, (n % d) * lanes_o + n // d] = 1.0
+    vmem = pl.BlockSpec(memory_space=pltpu.VMEM)
+    hbm = pl.BlockSpec(memory_space=pl.ANY)
+    xn = (windows, ca, block_len + K)
+    zs = (windows, ca, block_len)
     return pl.pallas_call(
-        gather_body(names, strips, blocks),
-        out_shape=jax.ShapeDtypeStruct((strips, blocks) + local.shape, local.dtype),
-        in_specs=[pl.BlockSpec(memory_space=pltpu.VMEM)],
-        out_specs=pl.BlockSpec(memory_space=pl.ANY),
-        scratch_shapes=[pltpu.SemaphoreType.DMA] + [pltpu.SemaphoreType.DMA((strips * blocks - 1,))] * 2,
+        gather_body(names, strips, blocks, wloc, block_len),
+        out_shape=[jax.ShapeDtypeStruct(xn, signal.dtype), jax.ShapeDtypeStruct(zs, signal.dtype)],
+        in_specs=[vmem] * 3,
+        out_specs=[hbm] * 2,
+        scratch_shapes=[
+            pltpu.VMEM((strips, blocks, 2, wloc, block_len), signal.dtype),
+            pltpu.VMEM(xn, signal.dtype),
+            pltpu.VMEM(zs, signal.dtype),
+            pltpu.SemaphoreType.DMA,
+            pltpu.SemaphoreType.DMA((strips * blocks - 1,)),
+            pltpu.SemaphoreType.DMA((strips, blocks)),
+            pltpu.SemaphoreType.DMA((strips, 2)),
+        ],
         compiler_params=pltpu.CompilerParams(collective_id=0, has_side_effects=True),
         name="gather_everywhere",
-    )(local)
+    )(signal, np.asarray(rows, jnp.bfloat16), np.asarray(lane, jnp.bfloat16))
 
 
 def per_device(names, signal):
@@ -314,14 +454,7 @@
     ca = 2 * blocks
     tab = tables(blocks, block_len)
 
-    every = gather_everywhere(signal.reshape(2 * wloc, block_len), names, strips, blocks)
-    x = every.reshape(strips, blocks, 2, wloc, block_len).transpose(0, 3, 2, 1, 4)
-    x = x.reshape(windows, 2, blocks, block_len)
-    halo = jnp.concatenate([x[:, :, 1:, :K], jnp.zeros((windows, 2, 1, K), x.dtype)], axis=2)
-    xn = jnp.concatenate([x, halo], axis=3).reshape(windows, ca, block_len + K)
-    zs = xn[:, :, K // 2 : K // 2 + block_len].reshape(windows, ca, 2, HALF, d)
-    zs = zs.transpose(0, 1, 2, 4, 3).reshape(windows, ca, block_len)
-
+    xn, zs = gather_everywhere(signal, names, strips, blocks)
     group = min(8, chan)
     vmem = pl.BlockSpec(memory_space=pltpu.VMEM)
     hbm = pl.BlockSpec(memory_space=pl.ANY)
@@ -337,8 +470,8 @@
             pltpu.VMEM((4, chan, HALF), jnp.float32),
             pltpu.VMEM((2, blocks, block_len), jnp.float32),
             pltpu.VMEM((d, 2, chan, HALF), jnp.float32),
-            pltpu.VMEM((2, ALT + J, J), jnp.bfloat16),
-            pltpu.VMEM((d, 4, chan * windows, HALF), jnp.float32),
+            pltpu.VMEM((2, 2, ALT + J, J), jnp.bfloat16),
+            pltpu.VMEM((d, 4, chan * (windows + 1), HALF), jnp.float32),
             pltpu.VMEM((2, 2, group, windows, block_len), jnp.bfloat16),
             pltpu.SemaphoreType.DMA((4,)),
             pltpu.SemaphoreType.DMA((2,)),

time: 104 us -> 51.9 us (0.50)
  the two profiles are of different devices: /device:TPU:15 before, /device:TPU:0 now
where the time goes in v2:
time: 51.9 us; the launch traced here: 51 us
  Pallas kernels  51 us (98%)
    pallas_call x1, Pallas kernels, per_device(): pl.pallas_call(main_body(windows, blocks, block_len, chan, group), in_spe...  32 us
    pallas_call x1, Pallas kernels, gather_everywhere(): pl.pallas_call(gather_body(names, strips, blocks, wloc, block_len), out_s...  19 us

profile of v2, /device:TPU:0, one launch (start us, length us, event | category | flops | bytes accessed | tf_op | source)
XLA Modules:
  0.0 51.0 jit_solution(10989042323712269274)
XLA Ops:
  0.0 19.0 %gather_everywhere.1 = (bf16[16,16,2304]{2,1,0:T(8,128)(2,1)}, bf16[16,16,2048]{2,1,0:T(8,128)(2,1)}) custom-call(bf16[2,4,2048]{2,1,0:T(4,128)(2,1)} %local_ref.1, bf16[2,64,64]{2,1,0:T(8,128)(2,1)} %constant.20.clone.rows_ref, bf16[256,256]{1,0:T(8,128)(2,1)} %constant.21.clone.lane_ref), custom_call_target="tpu_custom_call" | custom-call | tf_op jit(solution)/shard_map/gather_everywhere/pallas_call | solution.py:428
  19.0 32.0 %strip_windows.1 = bf16[2,64,16,2048]{3,2,1,0:T(8,128)(2,1)} custom-call(bf16[16,16,2304]{2,1,0:T(8,128)(2,1)} %get-tuple-element.7.xn_ref, bf16[16,16,2048]{2,1,0:T(8,128)(2,1)} %get-tuple-element.8.zs_ref, bf16[256,256]{1,0:T(8,128)(2,1)} %constant.22.clone.slot_ref, f32[8,256,128]{2,1,0:T(8,128)} %constant.23.clone.weight_ref, ...), custom_call_target="tpu_custom_call" | custom-call | tf_op jit(solution)/shard_map/strip_windows/pallas_call | solution.py:461

commit v3 on v1

v3 whole, which is shorter than its diff:
```python
import functools
import math

import jax
import jax.numpy as jnp
import numpy as np
from jax import lax
from jax.experimental import pallas as pl
from jax.experimental.pallas import tpu as pltpu
from jax.sharding import PartitionSpec as P

K = 256
J = 256
HALF = 128
ALT = 64
UNROLL = 2
GROUP = 8
TWO_PI = 2.0 * math.pi


def pair(phases, modulus):
    angles = TWO_PI * (phases % modulus) / modulus
    return np.cos(angles), np.sin(angles)


def small_dft(values):
    count = len(values)
    if count == 1:
        return values
    even = small_dft(values[0::2])
    odd = small_dft(values[1::2])
    low, high = [], []
    for i in range(count // 2):
        er, ei = even[i]
        orr, oi = odd[i]
        if i == 0:
            tr, ti = orr, oi
        elif 4 * i == count:
            tr, ti = oi, -orr
        else:
            c = math.cos(TWO_PI * i / count)
            s = math.sin(TWO_PI * i / count)
            if abs(c - s) < 1e-6:
                tr, ti = (orr + oi) * c, (oi - orr) * c
            elif abs(c + s) < 1e-6:
                tr, ti = (oi - orr) * s, (orr + oi) * (-s)
            else:
                tr, ti = orr * c + oi * s, oi * c - orr * s
        low.append((er + tr, ei + ti))
        high.append((er - tr, ei - ti))
    return low + high


def tables(blocks, block_len):
    d = block_len // J
    slots = J // (2 * blocks)
    total = blocks * block_len
    scale = 1.0 / math.sqrt(total * K)
    order = (
        HALF * d * np.arange(2)[:, None, None]
        + np.arange(d)[None, :, None]
        + d * np.arange(HALF)[None, None, :]
    ).reshape(-1)
    residues = np.arange(blocks)
    c, s = pair(residues[:, None] * order[None, :], total)
    lanes = np.stack([c, -s], axis=1) * scale
    c, s = pair(residues[:, None] * residues[None, :], blocks)
    folds = np.stack([c, -s], axis=1)[..., None] * np.ones(128)
    lane = np.arange(J)
    slot_of = (lane % HALF) // blocks
    slot = (np.arange(J) // (2 * blocks))[:, None] == slot_of[None, :]
    j = np.arange(HALF)
    b = d * j[None, :] + np.arange(d)[:, None]
    row = np.arange(J)
    lag = (row[None, :, None] - b[:, None, :]) % K
    start = ALT * (j // blocks)
    inside = (row[:, None] - start[None, :]) % K
    late = inside[None] < (b - start[None, :])[:, None, :]
    weight = 0.54 - 0.46 * np.cos(TWO_PI * lag / K)
    weight = np.stack([np.where(late, 0.0, weight), np.where(late, -weight, 0.0)], axis=1)
    chan = np.arange(K)
    c, s = pair(chan[:, None] * row[None, :], K)
    emat = np.stack([np.concatenate([c, s], 1), np.concatenate([-s, c], 1)])
    c, s = pair(chan[:, None] * (d * j)[None, :], K)
    c1, s1 = pair(chan[:, None] * np.ones((1, HALF), np.int64), K)
    phase = np.stack([c, s, c1, s1])
    c, s = pair(row[:, None] * row[None, :], J)
    dft = np.concatenate([np.concatenate([c, -s], 1), np.concatenate([s, c], 1)], 0)
    twid = np.stack(pair(np.arange(d)[:, None] * row[None, :], block_len))
    f32 = lambda v: np.asarray(v, np.float32)
    b16 = lambda v: np.asarray(np.asarray(v, np.float32), jnp.bfloat16)
    return dict(
        lanes=f32(lanes), folds=f32(folds), slot=b16(slot), weight=b16(weight),
        emat=b16(emat), phase=f32(phase), dft=b16(dft), twid=f32(twid),
    )


def in_hbm(value):
    return pltpu.with_memory_space_constraint(jnp.asarray(value), pltpu.HBM)


def first_body(names, strips, blocks, wloc, block_len, chan):
    d = block_len // J
    ca = 2 * blocks
    slots = J // ca
    halves = block_len // 2
    pairs = blocks // 2
    lanes_o = J // d
    count = ca * wloc

    def body(
        local_hbm, rows_hbm, lane_hbm, slot_hbm,
        weight_hbm, lanes_hbm, folds_hbm, emat_hbm, phase_hbm, g_ref,
        local_ref, rows_ref, lane_ref, slot_ref,
        every_ref, next_xn_ref, next_zs_ref, xn_ref, zs_ref, lhs_ref,
        weight_ref, lanes_ref, folds_ref, emat_ref, phase_ref, turn_ref, spin_ref,
        load_sem, direct_sem, relay_sem, hand_sem, recv_sem,
    ):
        s = lax.axis_index("strip")
        t = lax.axis_index("tm")
        other = t + 1 - 2 * lax.rem(t, 2)

        def device(strip, tm):
            where = {"strip": strip, "tm": tm}
            return tuple(where[name] for name in names)

        def strip_at(ds):
            return lax.rem(s + strips - ds, strips)

        def mate(dt):
            return lax.rem(t + blocks - 2 * dt, blocks)

        def rival(dt):
            return lax.rem(other + blocks - 2 * dt, blocks)

        across = [device(strip_at(strips - ds), t) for ds in range(1, strips)]
        inside = [device(s, mate(dt)) for dt in range(1, pairs)] + [device(s, other)]
        barrier = pltpu.get_barrier_semaphore()
        for peer in across + inside:
            pl.semaphore_signal(barrier, inc=1, device_id=peer, device_id_type=pl.DeviceIdType.MESH)
        local = pltpu.make_async_copy(local_hbm, local_ref, load_sem.at[8])
        local.start()
        loads = [
            pltpu.make_async_copy(rows_hbm, rows_ref, load_sem.at[5]),
            pltpu.make_async_copy(lane_hbm, lane_ref, load_sem.at[6]),
            pltpu.make_async_copy(slot_hbm, slot_ref, load_sem.at[7]),
            pltpu.make_async_copy(lanes_hbm.at[t], lanes_ref, load_sem.at[0]),
            pltpu.make_async_copy(folds_hbm.at[t], folds_ref, load_sem.at[1]),
            pltpu.make_async_copy(emat_hbm.at[:, pl.ds(s * chan, chan)], emat_ref, load_sem.at[2]),
            pltpu.make_async_copy(phase_hbm.at[:, pl.ds(s * chan, chan)], phase_ref, load_sem.at[3]),
            pltpu.make_async_copy(weight_hbm, weight_ref, load_sem.at[4]),
        ]
        for load in loads:
            load.start()
        local.wait()
        every_ref[s, t] = jnp.concatenate(
            [local_ref[0].astype(jnp.float32), local_ref[1].astype(jnp.float32)], axis=0
        ).astype(jnp.bfloat16)
        pl.semaphore_wait(barrier, len(across) + len(inside))

        def transfer(strip, tm, peer, send_sem):
            return pltpu.make_async_remote_copy(
                src_ref=every_ref.at[strip, tm],
                dst_ref=every_ref.at[strip, tm],
                send_sem=send_sem,
                recv_sem=recv_sem.at[strip, tm],
                device_id=peer,
                device_id_type=pl.DeviceIdType.MESH,
            )

        def arrived(strip, tm):
            transfer(strip, tm, inside[-1], direct_sem.at[0]).wait_recv()

        def direct(i):
            return transfer(s, t, (across + inside)[i], direct_sem.at[i])

        def relay(ds, i):
            return transfer(strip_at(ds), t, inside[i], relay_sem.at[ds, i])

        def hand(ds, dt):
            return transfer(strip_at(ds), mate(dt), inside[-1], hand_sem.at[ds, dt])

        def relay_all(ds):
            arrived(strip_at(ds), t)
            for i in range(len(inside)):
                relay(ds, i).start()

        def hand_over(ds):
            for dt in range(1, pairs):
                arrived(strip_at(ds), mate(dt))
                hand(ds, dt).start()

        def complete(ds):
            for dt in range(pairs):
                arrived(strip_at(ds), rival(dt))

        for i in range(len(across) + len(inside)):
            direct(i).start()

        low = lax.broadcasted_iota(jnp.int32, (ca, HALF), 1) < ALT

        def rows_of(ds):
            flat = every_ref[strip_at(ds)].reshape(count, block_len)
            nat = jnp.dot(rows_ref[0], flat, preferred_element_type=jnp.float32).astype(jnp.bfloat16)
            halo = jnp.dot(rows_ref[1], flat[:, :K], preferred_element_type=jnp.float32).astype(jnp.bfloat16)
            for wl in range(wloc):
                next_xn_ref[wl, :, :block_len] = nat[wl * ca : (wl + 1) * ca]
                next_xn_ref[wl, :, block_len:] = halo[wl * ca : (wl + 1) * ca]
            return jnp.concatenate([nat[:, HALF:], halo[:, :HALF]], axis=1)

        def lanes_of(full):
            moved = jnp.concatenate([full[:, q * J : (q + 1) * J] for q in range(block_len // J)], axis=0)
            moved = jnp.dot(moved, lane_ref[...], preferred_element_type=jnp.float32)
            for h in range(2):
                for o in range(d):
                    lanes = slice(o * lanes_o, (o + 1) * lanes_o)
                    part = jnp.concatenate(
                        [
                            moved[q * count : (q + 1) * count, lanes]
                            for q in range(h * d // 2, (h + 1) * d // 2)
                        ],
                        axis=1,
                    ).astype(jnp.bfloat16)
                    for wl in range(wloc):
                        next_zs_ref[wl, :, (h * d + o) * HALF : (h * d + o + 1) * HALF] = part[
                            wl * ca : (wl + 1) * ca
                        ]

        def build(src_ref, wl, slot):
            def lane_tile(v):
                return src_ref[wl, :, v * 128 : (v + 1) * 128].astype(jnp.float32)

            for h in range(2):
                left, right, late = [], [], []
                for part in range(slots):
                    g = (HALF * d * h) // ALT + part
                    picks = [(g + (c - g) % 4) // 2 for c in range(4)]
                    for side, dst in ((0, left), (1, right)):
                        v0, v1 = picks[2 * side], picks[2 * side + 1]
                        x0 = lane_tile(v0)
                        dst.append(x0 if v0 == v1 else jnp.where(low, x0, lane_tile(v1)))
                    n = g + 4
                    tail = lane_tile(n // 2)
                    if n % 2:
                        tail = pltpu.roll(tail, ALT, 1)
                    late.append(-tail)
                lhs_ref[slot, h, 0:ALT] = jnp.concatenate(late, axis=0).T[:ALT].astype(jnp.bfloat16)
                lhs_ref[slot, h, ALT : ALT + HALF] = jnp.concatenate(left, axis=0).T.astype(jnp.bfloat16)
                lhs_ref[slot, h, ALT + HALF :] = jnp.concatenate(right, axis=0).T.astype(jnp.bfloat16)

        def lag_products(wl, h, o):
            at = slice(h * halves + o * HALF, h * halves + (o + 2) * HALF)
            xs = zs_ref[wl, :, at].astype(jnp.float32)
            xr, xi = xs[:blocks], xs[blocks:]
            er, ei = turn_ref[0, :, at], turn_ref[1, :, at]
            zr = xr * er + xi * ei
            zi = xr * ei - xi * er
            mask = slot_ref[...]
            zre = jnp.concatenate([zr, -zi], axis=0).astype(jnp.bfloat16)
            zim = jnp.concatenate([zi, zr], axis=0).astype(jnp.bfloat16)
            rhs = jnp.concatenate(
                [
                    jnp.concatenate([zre] * slots, axis=0) * mask,
                    jnp.concatenate([zim] * slots, axis=0) * mask,
                ],
                axis=1,
            )
            return jnp.dot(lhs_ref[wl % 2, h], rhs, preferred_element_type=jnp.float32)

        def channels(ds, wl, h, o, lags):
            w = strip_at(ds) * wloc + wl
            emat = emat_ref[...].reshape(2 * chan, 2 * J)
            cols = []
            for c in range(2):
                for oo in range(2):
                    lanes = slice(c * J + oo * HALF, c * J + (oo + 1) * HALF)
                    late = lags[:ALT, lanes].astype(jnp.bfloat16)
                    parts = []
                    for q in range(4):
                        at = slice(q * ALT, (q + 1) * ALT)
                        early = lags[(q + 1) * ALT : (q + 2) * ALT, lanes].astype(jnp.bfloat16)
                        parts.append(early * weight_ref[o + oo, 0, at] + late * weight_ref[o + oo, 1, at])
                    cols.append(jnp.concatenate(parts, axis=0))
            taps = jnp.concatenate(
                [jnp.concatenate(cols[:2], axis=1), jnp.concatenate(cols[2:], axis=1)], axis=0
            )
            y = jnp.dot(emat, taps, preferred_element_type=jnp.float32)
            for oo in range(2):
                lanes = slice(oo * HALF, (oo + 1) * HALF)
                yr, yi = y[:chan, lanes], y[chan:, lanes]
                c, sn = spin_ref[o + oo, 0], spin_ref[o + oo, 1]
                gr = (yr * c - yi * sn).astype(jnp.bfloat16).reshape(chan // GROUP, GROUP, HALF)
                gi = (yr * sn + yi * c).astype(jnp.bfloat16).reshape(chan // GROUP, GROUP, HALF)
                g_ref[:, w, o + oo, :, h * HALF : (h + 1) * HALF] = gr
                g_ref[:, w, o + oo, :, J + h * HALF : J + (h + 1) * HALF] = gi

        near = [1, strips - 1] if strips > 2 else [1]
        far = [ds for ds in range(1, strips) if ds not in near]
        for ds in near:
            relay_all(ds)
        hand_over(0)
        for ds in far:
            relay_all(ds)

        for load in loads:
            load.wait()
        br, bi = lanes_ref[0:1], lanes_ref[1:2]
        for q in range(block_len // 128):
            at = slice(q * 128, (q + 1) * 128)
            fr, fi = folds_ref[0], folds_ref[1]
            turn_ref[0, :, at] = fr * br[:, at] - fi * bi[:, at]
            turn_ref[1, :, at] = fr * bi[:, at] + fi * br[:, at]
        gr, gi = phase_ref[0], phase_ref[1]
        for o in range(d):
            if o > 0:
                gr, gi = gr * phase_ref[2] - gi * phase_ref[3], gr * phase_ref[3] + gi * phase_ref[2]
            spin_ref[o, 0] = gr
            spin_ref[o, 1] = gi

        complete(0)
        lanes_of(rows_of(0))
        build(next_xn_ref, 0, 0)

        @pl.loop(0, strips)
        def _(ds):
            xn_ref[...] = next_xn_ref[...]
            zs_ref[...] = next_zs_ref[...]
            after = jnp.minimum(ds + 1, strips - 1)

            @pl.when(ds + 1 < strips)
            def _():
                hand_over(ds + 1)

            for first in range(0, wloc, UNROLL):
                last = first + UNROLL >= wloc
                mine = range(first, min(first + UNROLL, wloc))

                if last:

                    @pl.when(ds + 1 < strips)
                    def _():
                        complete(ds + 1)

                    full = rows_of(after)
                pending = None
                for wl in mine:
                    if wl + 1 < wloc:
                        build(xn_ref, wl + 1, (wl + 1) % 2)
                    else:
                        build(next_xn_ref, 0, 0)
                    for h in range(2):
                        for o in range(0, d, 2):
                            lags = lag_products(wl, h, o)
                            if pending is not None:
                                channels(*pending)
                            pending = (ds, wl, h, o, lags)
                        if last and wl == first and h == 0:
                            lanes_of(full)
                channels(*pending)

        for i in range(len(across) + len(inside)):
            direct(i).wait_send()
        for ds in range(strips):
            if ds > 0:
                for i in range(len(inside)):
                    relay(ds, i).wait_send()
            for dt in range(1, pairs):
                hand(ds, dt).wait_send()

    return body


def arrangements(blocks, wloc, d):
    count = 2 * blocks * wloc
    w, c, a = np.meshgrid(np.arange(wloc), np.arange(2), np.arange(blocks), indexing="ij")
    target = ((w * 2 + c) * blocks + a).reshape(-1)
    source = ((a * 2 + c) * wloc + w).reshape(-1)
    rows = np.zeros((2, count, count))
    rows[0, target, source] = 1.0
    inner = a.reshape(-1) + 1 < blocks
    rows[1, target[inner], source[inner] + 2 * wloc] = 1.0
    lane = np.zeros((J, J))
    n = np.arange(J)
    lane[n, (n % d) * (J // d) + n // d] = 1.0
    return np.asarray(rows, jnp.bfloat16), np.asarray(lane, jnp.bfloat16)


def first_phase(signal, tab, names, strips, blocks):
    wloc, block_len = signal.shape[1], signal.shape[2]
    d = block_len // J
    chan = K // strips
    windows = wloc * strips
    ca = 2 * blocks
    rows, lane = arrangements(blocks, wloc, d)
    hbm = pl.BlockSpec(memory_space=pltpu.HBM)
    b16, f32 = jnp.bfloat16, jnp.float32
    peers = strips - 1 + blocks // 2
    return pl.pallas_call(
        first_body(names, strips, blocks, wloc, block_len, chan),
        out_shape=pltpu.VMEM((chan // GROUP, windows, d, GROUP, 2 * J), b16),
        in_specs=[hbm] * 9,
        out_specs=pl.BlockSpec(memory_space=pltpu.VMEM),
        scratch_shapes=[
            pltpu.VMEM((2, wloc, block_len), b16),
            pltpu.VMEM((2, ca * wloc, ca * wloc), b16),
            pltpu.VMEM((J, J), b16),
            pltpu.VMEM((J, J), b16),
            pltpu.VMEM((strips, blocks, 2 * wloc, block_len), b16),
            pltpu.VMEM((wloc, ca, block_len + K), b16),
            pltpu.VMEM((wloc, ca, block_len), b16),
            pltpu.VMEM((wloc, ca, block_len + K), b16),
            pltpu.VMEM((wloc, ca, block_len), b16),
            pltpu.VMEM((2, 2, ALT + J, J), b16),
            pltpu.VMEM((d, 2, J, HALF), b16),
            pltpu.VMEM((2, block_len), f32),
            pltpu.VMEM((2, blocks, 128), f32),
            pltpu.VMEM((2, chan, 2 * J), b16),
            pltpu.VMEM((4, chan, HALF), f32),
            pltpu.VMEM((2, blocks, block_len), f32),
            pltpu.VMEM((d, 2, chan, HALF), f32),
            pltpu.SemaphoreType.DMA((9,)),
            pltpu.SemaphoreType.DMA((peers,)),
            pltpu.SemaphoreType.DMA((strips, blocks // 2)),
            pltpu.SemaphoreType.DMA((strips, blocks // 2)),
            pltpu.SemaphoreType.DMA((strips, blocks)),
        ],
        compiler_params=pltpu.CompilerParams(
            collective_id=0, has_side_effects=True, vmem_limit_bytes=24 * 1024 * 1024
        ),
        name="lag_channels",
    )(*map(in_hbm, (signal, rows, lane, tab["slot"], tab["weight"], tab["lanes"], tab["folds"], tab["emat"], tab["phase"])))


def final_body(chunks, windows, block_len):
    d = block_len // J
    pitch = GROUP + 1
    step = 4
    span = 8
    unroll = 2 if chunks % 2 == 0 else 1

    def body(g_ref, dft_hbm, twid_hbm, out_hbm, dft_ref, twid_ref, out_ref, y_ref, table_sem, out_sem):
        def write(i):
            at = pl.ds(i * GROUP, GROUP)
            return pltpu.make_async_copy(out_ref.at[:, at], out_hbm.at[:, at], out_sem.at[i])

        tables_in = [
            pltpu.make_async_copy(dft_hbm, dft_ref, table_sem.at[0]),
            pltpu.make_async_copy(twid_hbm, twid_ref, table_sem.at[1]),
        ]
        for copy in tables_in:
            copy.start()
        for copy in tables_in:
            copy.wait()

        def windows_of(i, u, w0):
            count = step * GROUP
            lhs = jnp.concatenate(
                [g_ref[i, w0 : w0 + step, o].reshape(count, 2 * J) for o in range(d)], axis=0
            )
            inner = jnp.dot(lhs, dft_ref[...], preferred_element_type=jnp.float32)
            turned = []
            for o in range(d):
                vr = inner[o * count : (o + 1) * count, :J]
                vi = inner[o * count : (o + 1) * count, J:]
                if o > 0:
                    tc, ts = twid_ref[0, o : o + 1], twid_ref[1, o : o + 1]
                    vr, vi = vr * tc + vi * ts, vi * tc - vr * ts
                turned.append((vr, vi))
            for m, both in enumerate(small_dft(turned)):
                for c in range(2):
                    for q in range(J // 128):
                        for wi in range(step):
                            y_ref[u, c, m * (J // 128) + q, pl.ds((w0 + wi) * pitch, GROUP), :] = both[c][
                                wi * GROUP : (wi + 1) * GROUP, q * 128 : (q + 1) * 128
                            ]
            if (w0 + step) % span == 0:
                w1 = w0 + step - span
                for k in range(GROUP):
                    for c in range(2):
                        for q in range(block_len // 128):
                            out_ref[c, i * GROUP + k, w1 : w1 + span, q * 128 : (q + 1) * 128] = y_ref[
                                u, c, q, pl.ds(w1 * pitch + k, span, stride=pitch), :
                            ].astype(jnp.bfloat16)

        @pl.loop(0, chunks // unroll)
        def _(n):
            for u in range(unroll):
                for w0 in range(0, windows, step):
                    windows_of(n * unroll + u, u, w0)
            for u in range(unroll):
                write(n * unroll + u).start()

        @pl.loop(0, chunks)
        def _(i):
            write(i).wait()

    return body


def final_phase(g, tab):
    chunks, windows, d, _, wide = g.shape
    block_len = d * J
    chan = chunks * GROUP
    hbm = pl.BlockSpec(memory_space=pltpu.HBM)
    b16, f32 = jnp.bfloat16, jnp.float32
    return pl.pallas_call(
        final_body(chunks, windows, block_len),
        in_specs=[pl.BlockSpec(memory_space=pltpu.VMEM), hbm, hbm],
        out_specs=hbm,
        out_shape=jax.ShapeDtypeStruct((2, chan, windows, block_len), b16),
        scratch_shapes=[
            pltpu.VMEM((wide, wide), b16),
            pltpu.VMEM((2, d, J), f32),
            pltpu.VMEM((2, chan, windows, block_len), b16),
            pltpu.VMEM((2, 2, block_len // 128, windows * (GROUP + 1), 128), f32),
            pltpu.SemaphoreType.DMA((2,)),
            pltpu.SemaphoreType.DMA((chunks,)),
        ],
        compiler_params=pltpu.CompilerParams(vmem_limit_bytes=28 * 1024 * 1024),
        name="frequencies",
    )(pltpu.with_memory_space_constraint(g, pltpu.VMEM), in_hbm(tab["dft"]), in_hbm(tab["twid"]))


def per_device(names, signal):
    blocks = lax.axis_size("tm")
    strips = lax.axis_size("strip")
    wloc, block_len = signal.shape[1], signal.shape[2]
    tab = tables(blocks, block_len)
    g = first_phase(signal, tab, names, strips, blocks)
    out = final_phase(g, tab)
    return out.reshape(2, K // strips, wloc * strips, 1, block_len)


def solution(mesh):
    return jax.shard_map(
        functools.partial(per_device, tuple(mesh.axis_names)),
        mesh=mesh,
        in_specs=(P(None, "strip", "tm"),),
        out_specs=P(None, "strip", None, "tm", None),
        check_vma=False,
    )
```

time: 104 us -> 44.9 us (0.43)
  the two profiles are of different devices: /device:TPU:15 before, /device:TPU:0 now
where the time goes in v3:
time: 44.9 us; the launch traced here: 44.7 us
  Pallas kernels  44.7 us (100%)
    pallas_call x1, Pallas kernels, first_phase(): pl.pallas_call(first_body(names, strips, blocks, wloc, block_len, chan),...  33.4 us
    pallas_call x1, Pallas kernels, final_phase(): pl.pallas_call(final_body(chunks, windows, block_len), in_specs=[pl.Block...  11.3 us

profile of v3, /device:TPU:0, one launch (start us, length us, event | category | flops | bytes accessed | tf_op | source)
XLA Modules:
  0.0 44.7 jit_solution(13864657151133569423)
XLA Ops:
  0.0 33.4 %lag_channels.1.g_ref = bf16[8,16,8,8,512]{4,3,2,1,0:T(8,128)(2,1)S(1)} custom-call(bf16[2,4,2048]{2,1,0:T(4,128)(2,1)} %local_hbm.1, bf16[2,64,64]{2,1,0:T(8,128)(2,1)} %constant.20.clone.rows_hbm, bf16[256,256]{1,0:T(8,128)(2,1)} %constant.21.clone.lane_hbm, bf16[256,256]{1,0:T(8,128)(2,1)} %constant.22.clone.slot_hbm, ...), custom_call_target="tpu_custom_call" | custom-call | tf_op jit(solution)/shard_map/lag_channels/pallas_call | solution.py:398
  33.5 11.3 %frequencies.1 = bf16[2,64,16,2048]{3,2,1,0:T(8,128)(2,1)} custom-call(bf16[8,16,8,8,512]{4,3,2,1,0:T(8,128)(2,1)S(1)} %lag_channels.1.g_ref, bf16[512,512]{1,0:T(8,128)(2,1)} %constant.28.clone.dft_hbm, f32[2,8,256]{2,1,0:T(8,128)} %constant.29.clone.twid_hbm), custom_call_target="tpu_custom_call" | custom-call | tf_op jit(solution)/shard_map/frequencies/pallas_call | solution.py:506

commit v4 on v3

--- a/solution.py
+++ b/solution.py
@@ -77,7 +77,7 @@
     inside = (row[:, None] - start[None, :]) % K
     late = inside[None] < (b - start[None, :])[:, None, :]
     weight = 0.54 - 0.46 * np.cos(TWO_PI * lag / K)
-    weight = np.stack([np.where(late, 0.0, weight), np.where(late, -weight, 0.0)], axis=1)
+    weight = np.where(late, -weight, weight)
     chan = np.arange(K)
     c, s = pair(chan[:, None] * row[None, :], K)
     emat = np.stack([np.concatenate([c, s], 1), np.concatenate([-s, c], 1)])
@@ -85,7 +85,10 @@
     c1, s1 = pair(chan[:, None] * np.ones((1, HALF), np.int64), K)
     phase = np.stack([c, s, c1, s1])
     c, s = pair(row[:, None] * row[None, :], J)
-    dft = np.concatenate([np.concatenate([c, -s], 1), np.concatenate([s, c], 1)], 0)
+    real, imag = np.concatenate([c, s], 0), np.concatenate([-s, c], 0)
+    dft = np.concatenate(
+        [part[:, q * HALF : (q + 1) * HALF] for q in range(2) for part in (real, imag)], 1
+    )
     twid = np.stack(pair(np.arange(d)[:, None] * row[None, :], block_len))
     f32 = lambda v: np.asarray(v, np.float32)
     b16 = lambda v: np.asarray(np.asarray(v, np.float32), jnp.bfloat16)
@@ -97,6 +100,10 @@
 
 def in_hbm(value):
     return pltpu.with_memory_space_constraint(jnp.asarray(value), pltpu.HBM)
+
+
+def in_vmem(value):
+    return pltpu.with_memory_space_constraint(jnp.asarray(value), pltpu.VMEM)
 
 
 def first_body(names, strips, blocks, wloc, block_len, chan):
@@ -113,7 +120,7 @@
         weight_hbm, lanes_hbm, folds_hbm, emat_hbm, phase_hbm, g_ref,
         local_ref, rows_ref, lane_ref, slot_ref,
         every_ref, next_xn_ref, next_zs_ref, xn_ref, zs_ref, lhs_ref,
-        weight_ref, lanes_ref, folds_ref, emat_ref, phase_ref, turn_ref, spin_ref,
+        signed_ref, weight_ref, taps_ref, lanes_ref, folds_ref, emat_ref, phase_ref, turn_ref, spin_ref,
         load_sem, direct_sem, relay_sem, hand_sem, recv_sem,
     ):
         s = lax.axis_index("strip")
@@ -148,7 +155,7 @@
             pltpu.make_async_copy(folds_hbm.at[t], folds_ref, load_sem.at[1]),
             pltpu.make_async_copy(emat_hbm.at[:, pl.ds(s * chan, chan)], emat_ref, load_sem.at[2]),
             pltpu.make_async_copy(phase_hbm.at[:, pl.ds(s * chan, chan)], phase_ref, load_sem.at[3]),
-            pltpu.make_async_copy(weight_hbm, weight_ref, load_sem.at[4]),
+            pltpu.make_async_copy(weight_hbm, signed_ref, load_sem.at[4]),
         ]
         for load in loads:
             load.start()
@@ -194,7 +201,9 @@
             for dt in range(pairs):
                 arrived(strip_at(ds), rival(dt))
 
-        for i in range(len(across) + len(inside)):
+        for i in range(len(inside)):
+            direct(len(across) + i).start()
+        for i in range(len(across)):
             direct(i).start()
 
         low = lax.broadcasted_iota(jnp.int32, (ca, HALF), 1) < ALT
@@ -228,7 +237,7 @@
 
         def build(src_ref, wl, slot):
             def lane_tile(v):
-                return src_ref[wl, :, v * 128 : (v + 1) * 128].astype(jnp.float32)
+                return src_ref[wl, :, v * 128 : (v + 1) * 128]
 
             for h in range(2):
                 left, right, late = [], [], []
@@ -242,11 +251,11 @@
                     n = g + 4
                     tail = lane_tile(n // 2)
                     if n % 2:
-                        tail = pltpu.roll(tail, ALT, 1)
+                        tail = pltpu.roll(tail.astype(jnp.float32), ALT, 1).astype(jnp.bfloat16)
                     late.append(-tail)
-                lhs_ref[slot, h, 0:ALT] = jnp.concatenate(late, axis=0).T[:ALT].astype(jnp.bfloat16)
-                lhs_ref[slot, h, ALT : ALT + HALF] = jnp.concatenate(left, axis=0).T.astype(jnp.bfloat16)
-                lhs_ref[slot, h, ALT + HALF :] = jnp.concatenate(right, axis=0).T.astype(jnp.bfloat16)
+                lhs_ref[slot, h, 0:ALT] = jnp.concatenate(late, axis=0).T[:ALT]
+                lhs_ref[slot, h, ALT : ALT + HALF] = jnp.concatenate(left, axis=0).T
+                lhs_ref[slot, h, ALT + HALF :] = jnp.concatenate(right, axis=0).T
 
         def lag_products(wl, h, o):
             at = slice(h * halves + o * HALF, h * halves + (o + 2) * HALF)
@@ -267,9 +276,7 @@
             )
             return jnp.dot(lhs_ref[wl % 2, h], rhs, preferred_element_type=jnp.float32)
 
-        def channels(ds, wl, h, o, lags):
-            w = strip_at(ds) * wloc + wl
-            emat = emat_ref[...].reshape(2 * chan, 2 * J)
+        def weigh(o, lags):
             cols = []
             for c in range(2):
                 for oo in range(2):
@@ -281,9 +288,13 @@
                         early = lags[(q + 1) * ALT : (q + 2) * ALT, lanes].astype(jnp.bfloat16)
                         parts.append(early * weight_ref[o + oo, 0, at] + late * weight_ref[o + oo, 1, at])
                     cols.append(jnp.concatenate(parts, axis=0))
-            taps = jnp.concatenate(
+            return jnp.concatenate(
                 [jnp.concatenate(cols[:2], axis=1), jnp.concatenate(cols[2:], axis=1)], axis=0
             )
+
+        def channels(ds, wl, h, o, taps):
+            w = strip_at(ds) * wloc + wl
+            emat = emat_ref[...].reshape(2 * chan, 2 * J)
             y = jnp.dot(emat, taps, preferred_element_type=jnp.float32)
             for oo in range(2):
                 lanes = slice(oo * HALF, (oo + 1) * HALF)
@@ -294,16 +305,12 @@
                 g_ref[:, w, o + oo, :, h * HALF : (h + 1) * HALF] = gr
                 g_ref[:, w, o + oo, :, J + h * HALF : J + (h + 1) * HALF] = gi
 
-        near = [1, strips - 1] if strips > 2 else [1]
-        far = [ds for ds in range(1, strips) if ds not in near]
-        for ds in near:
-            relay_all(ds)
-        hand_over(0)
-        for ds in far:
-            relay_all(ds)
-
         for load in loads:
             load.wait()
+        for o in range(d):
+            signed = signed_ref[o].astype(jnp.float32)
+            weight_ref[o, 0] = jnp.maximum(signed, 0.0).astype(jnp.bfloat16)
+            weight_ref[o, 1] = jnp.minimum(signed, 0.0).astype(jnp.bfloat16)
         br, bi = lanes_ref[0:1], lanes_ref[1:2]
         for q in range(block_len // 128):
             at = slice(q * 128, (q + 1) * 128)
@@ -317,6 +324,12 @@
             spin_ref[o, 0] = gr
             spin_ref[o, 1] = gi
 
+        near = [1, strips - 1] if strips > 2 else [1]
+        far = [ds for ds in range(1, strips) if ds not in near]
+        hand_over(0)
+        for ds in near + far:
+            relay_all(ds)
+        taps_ref[...] = jnp.zeros((2 * J, J), jnp.bfloat16)
         complete(0)
         lanes_of(rows_of(0))
         build(next_xn_ref, 0, 0)
@@ -352,12 +365,17 @@
                         for o in range(0, d, 2):
                             lags = lag_products(wl, h, o)
                             if pending is not None:
-                                channels(*pending)
-                            pending = (ds, wl, h, o, lags)
+                                channels(ds, *pending[:3], weigh(*pending[2:]))
+                            elif first > 0:
+                                channels(ds, first - 1, 1, d - 2, taps_ref[...])
+                            else:
+                                channels(ds - 1, wloc - 1, 1, d - 2, taps_ref[...])
+                            pending = (wl, h, o, lags)
                         if last and wl == first and h == 0:
                             lanes_of(full)
-                channels(*pending)
-
+                taps_ref[...] = weigh(*pending[2:])
+
+        channels(strips - 1, wloc - 1, 1, d - 2, taps_ref[...])
         for i in range(len(across) + len(inside)):
             direct(i).wait_send()
         for ds in range(strips):
@@ -411,7 +429,9 @@
             pltpu.VMEM((wloc, ca, block_len + K), b16),
             pltpu.VMEM((wloc, ca, block_len), b16),
             pltpu.VMEM((2, 2, ALT + J, J), b16),
+            pltpu.VMEM((d, J, HALF), b16),
             pltpu.VMEM((d, 2, J, HALF), b16),
+            pltpu.VMEM((2 * J, J), b16),
             pltpu.VMEM((2, block_len), f32),
             pltpu.VMEM((2, blocks, 128), f32),
             pltpu.VMEM((2, chan, 2 * J), b16),
@@ -436,42 +456,36 @@
     pitch = GROUP + 1
     step = 4
     span = 8
-    unroll = 2 if chunks % 2 == 0 else 1
-
-    def body(g_ref, dft_hbm, twid_hbm, out_hbm, dft_ref, twid_ref, out_ref, y_ref, table_sem, out_sem):
+    unroll = 4 if chunks % 4 == 0 else 1
+
+    def body(g_ref, dft_ref, twid_ref, out_hbm, out_ref, y_ref, out_sem):
         def write(i):
             at = pl.ds(i * GROUP, GROUP)
             return pltpu.make_async_copy(out_ref.at[:, at], out_hbm.at[:, at], out_sem.at[i])
-
-        tables_in = [
-            pltpu.make_async_copy(dft_hbm, dft_ref, table_sem.at[0]),
-            pltpu.make_async_copy(twid_hbm, twid_ref, table_sem.at[1]),
-        ]
-        for copy in tables_in:
-            copy.start()
-        for copy in tables_in:
-            copy.wait()
 
         def windows_of(i, u, w0):
             count = step * GROUP
             lhs = jnp.concatenate(
                 [g_ref[i, w0 : w0 + step, o].reshape(count, 2 * J) for o in range(d)], axis=0
             )
-            inner = jnp.dot(lhs, dft_ref[...], preferred_element_type=jnp.float32)
-            turned = []
-            for o in range(d):
-                vr = inner[o * count : (o + 1) * count, :J]
-                vi = inner[o * count : (o + 1) * count, J:]
-                if o > 0:
-                    tc, ts = twid_ref[0, o : o + 1], twid_ref[1, o : o + 1]
-                    vr, vi = vr * tc + vi * ts, vi * tc - vr * ts
-                turned.append((vr, vi))
-            for m, both in enumerate(small_dft(turned)):
-                for c in range(2):
-                    for q in range(J // 128):
+            for q in range(2):
+                inner = jnp.dot(
+                    lhs, dft_ref[:, q * J : (q + 1) * J], preferred_element_type=jnp.float32
+                )
+                turned = []
+                for o in range(d):
+                    vr = inner[o * count : (o + 1) * count, :HALF]
+                    vi = inner[o * count : (o + 1) * count, HALF:]
+                    if o > 0:
+                        at = slice(q * HALF, (q + 1) * HALF)
+                        tc, ts = twid_ref[0, o : o + 1, at], twid_ref[1, o : o + 1, at]
+                        vr, vi = vr * tc + vi * ts, vi * tc - vr * ts
+                    turned.append((vr, vi))
+                for m, both in enumerate(small_dft(turned)):
+                    for c in range(2):
                         for wi in range(step):
-                            y_ref[u, c, m * (J // 128) + q, pl.ds((w0 + wi) * pitch, GROUP), :] = both[c][
-                                wi * GROUP : (wi + 1) * GROUP, q * 128 : (q + 1) * 128
+                            y_ref[u, c, m * 2 + q, pl.ds((w0 + wi) * pitch, GROUP), :] = both[c][
+                                wi * GROUP : (wi + 1) * GROUP
                             ]
             if (w0 + step) % span == 0:
                 w1 = w0 + step - span
@@ -486,8 +500,7 @@
         def _(n):
             for u in range(unroll):
                 for w0 in range(0, windows, step):
-                    windows_of(n * unroll + u, u, w0)
-            for u in range(unroll):
+                    windows_of(n * unroll + u, u % 2, w0)
                 write(n * unroll + u).start()
 
         @pl.loop(0, chunks)
@@ -505,20 +518,17 @@
     b16, f32 = jnp.bfloat16, jnp.float32
     return pl.pallas_call(
         final_body(chunks, windows, block_len),
-        in_specs=[pl.BlockSpec(memory_space=pltpu.VMEM), hbm, hbm],
+        in_specs=[pl.BlockSpec(memory_space=pltpu.VMEM)] * 3,
         out_specs=hbm,
         out_shape=jax.ShapeDtypeStruct((2, chan, windows, block_len), b16),
         scratch_shapes=[
-            pltpu.VMEM((wide, wide), b16),
-            pltpu.VMEM((2, d, J), f32),
             pltpu.VMEM((2, chan, windows, block_len), b16),
             pltpu.VMEM((2, 2, block_len // 128, windows * (GROUP + 1), 128), f32),
-            pltpu.SemaphoreType.DMA((2,)),
             pltpu.SemaphoreType.DMA((chunks,)),
         ],
         compiler_params=pltpu.CompilerParams(vmem_limit_bytes=28 * 1024 * 1024),
         name="frequencies",
-    )(pltpu.with_memory_space_constraint(g, pltpu.VMEM), in_hbm(tab["dft"]), in_hbm(tab["twid"]))
+    )(*map(in_vmem, (g, tab["dft"], tab["twid"])))
 
 
 def per_device(names, signal):

time: 44.9 us -> 42.6 us (0.949)
  Pallas kernels: 44.7 us -> 42.4 us
    pallas_call x1, Pallas kernels: 11.3 us -> 9.72 us  [final_phase(): pl.pallas_call(final_body(chunks, windows, block_len), in_specs=[pl.Block...]
    pallas_call x1, Pallas kernels: 33.4 us -> 32.7 us  [first_phase(): pl.pallas_call(first_body(names, strips, blocks, wloc, block_len, chan),...]
where the time goes in v4:
time: 42.6 us; the launch traced here: 42.4 us
  Pallas kernels  42.4 us (100%)
    pallas_call x1, Pallas kernels, first_phase(): pl.pallas_call(first_body(names, strips, blocks, wloc, block_len, chan),...  32.7 us
    pallas_call x1, Pallas kernels, final_phase(): pl.pallas_call(final_body(chunks, windows, block_len), in_specs=[pl.Block...  9.72 us

profile of v4, /device:TPU:0, one launch (start us, length us, event | category | flops | bytes accessed | tf_op | source)
XLA Modules:
  0.0 42.4 jit_solution(7710720765734030468)
XLA Ops:
  0.0 0.0 copy-start.1
  0.0 0.0 copy-start
  0.0 32.7 %lag_channels.1.g_ref = bf16[8,16,8,8,512]{4,3,2,1,0:T(8,128)(2,1)S(1)} custom-call(bf16[2,4,2048]{2,1,0:T(4,128)(2,1)} %local_hbm.1, bf16[2,64,64]{2,1,0:T(8,128)(2,1)} %constant.20.clone.rows_hbm, bf16[256,256]{1,0:T(8,128)(2,1)} %constant.21.clone.lane_hbm, bf16[256,256]{1,0:T(8,128)(2,1)} %constant.22.clone.slot_hbm, ...), custom_call_target="tpu_custom_call" | custom-call | tf_op jit(solution)/shard_map/lag_channels/pallas_call | solution.py:416
  32.7 0.0 copy-done.1
  32.7 0.0 copy-done
  32.7 9.7 %frequencies.1 = bf16[2,64,16,2048]{3,2,1,0:T(8,128)(2,1)} custom-call(bf16[8,16,8,8,512]{4,3,2,1,0:T(8,128)(2,1)S(1)} %lag_channels.1.g_ref, bf16[512,512]{1,0:T(8,128)(2,1)S(1)} %copy-done, f32[2,8,256]{2,1,0:T(8,128)S(1)} %copy-done.1), custom_call_target="tpu_custom_call" | custom-call | tf_op jit(solution)/shard_map/frequencies/pallas_call | solution.py:519
Async XLA Ops:
  0.0 32.7 %copy-start.1 = (f32[2,8,256]{2,1,0:T(8,128)S(1)}, f32[2,8,256]{2,1,0:T(8,128)}, u32[]{:S(2)}) copy-start(f32[2,8,256]{2,1,0:T(8,128)} %constant.29.clone.twid_ref) | copy-start | bytes 49156
  0.0 32.7 %copy-start = (bf16[512,512]{1,0:T(8,128)(2,1)S(1)}, bf16[512,512]{1,0:T(8,128)(2,1)}, u32[]{:S(2)}) copy-start(bf16[512,512]{1,0:T(8,128)(2,1)} %constant.28.clone.dft_ref) | copy-start | bytes 1572868

commit v5 on v4

--- a/solution.py
+++ b/solution.py
@@ -454,7 +454,7 @@
 def final_body(chunks, windows, block_len):
     d = block_len // J
     pitch = GROUP + 1
-    step = 4
+    step = 8
     span = 8
     unroll = 4 if chunks % 4 == 0 else 1
 

time: 42.6 us -> 42.3 us (level)
  no operation moved by 1% of the time
where the time goes in v5:
time: 42.3 us; the launch traced here: 42.1 us
  Pallas kernels  42.1 us (100%)
    pallas_call x1, Pallas kernels, first_phase(): pl.pallas_call(first_body(names, strips, blocks, wloc, block_len, chan),...  32.7 us
    pallas_call x1, Pallas kernels, final_phase(): pl.pallas_call(final_body(chunks, windows, block_len), in_specs=[pl.Block...  9.43 us

profile of v5, /device:TPU:0, one launch (start us, length us, event | category | flops | bytes accessed | tf_op | source)
XLA Modules:
  0.0 42.1 jit_solution(4174893584862439473)
XLA Ops:
  0.0 0.0 copy-start.1
  0.0 0.0 copy-start
  0.0 32.7 %lag_channels.1.g_ref = bf16[8,16,8,8,512]{4,3,2,1,0:T(8,128)(2,1)S(1)} custom-call(bf16[2,4,2048]{2,1,0:T(4,128)(2,1)} %local_hbm.1, bf16[2,64,64]{2,1,0:T(8,128)(2,1)} %constant.20.clone.rows_hbm, bf16[256,256]{1,0:T(8,128)(2,1)} %constant.21.clone.lane_hbm, bf16[256,256]{1,0:T(8,128)(2,1)} %constant.22.clone.slot_hbm, ...), custom_call_target="tpu_custom_call" | custom-call | tf_op jit(solution)/shard_map/lag_channels/pallas_call | solution.py:416
  32.7 0.0 copy-done.1
  32.7 0.0 copy-done
  32.7 9.4 %frequencies.1 = bf16[2,64,16,2048]{3,2,1,0:T(8,128)(2,1)} custom-call(bf16[8,16,8,8,512]{4,3,2,1,0:T(8,128)(2,1)S(1)} %lag_channels.1.g_ref, bf16[512,512]{1,0:T(8,128)(2,1)S(1)} %copy-done, f32[2,8,256]{2,1,0:T(8,128)S(1)} %copy-done.1), custom_call_target="tpu_custom_call" | custom-call | tf_op jit(solution)/shard_map/frequencies/pallas_call | solution.py:519
Async XLA Ops:
  0.0 32.7 %copy-start.1 = (f32[2,8,256]{2,1,0:T(8,128)S(1)}, f32[2,8,256]{2,1,0:T(8,128)}, u32[]{:S(2)}) copy-start(f32[2,8,256]{2,1,0:T(8,128)} %constant.29.clone.twid_ref) | copy-start | bytes 49156
  0.0 32.7 %copy-start = (bf16[512,512]{1,0:T(8,128)(2,1)S(1)}, bf16[512,512]{1,0:T(8,128)(2,1)}, u32[]{:S(2)}) copy-start(bf16[512,512]{1,0:T(8,128)(2,1)} %constant.28.clone.dft_ref) | copy-start | bytes 1572868
